TPU v7x, 32 devices: a whole 2x2x4 slice. The times are simulated.
32 devices in a mesh: section: 2 (over core), row: 4 (over y, x), col: 4 (over z).
Axes of the slice: x: 2, y: 2, z: 4, core: 2. Of those that a mesh axis runs over, the one named last changes fastest.
Arguments:
- section_inputs: bfloat16 [2, 2, 48, 4096], P('section', None, 'col', 'row'), may hold values from -6 to 6
- out_grad: bfloat16 [2, 48, 4096], P(None, 'col', 'row'), may hold values from -6 to 6
- gate_weight: bfloat16 [2, 4096, 14336], P('section', 'row', 'col'), may hold values from -0.09375 to 0.09375
- up_weight: bfloat16 [2, 4096, 14336], P('section', 'row', 'col'), may hold values from -0.09375 to 0.09375
- down_weight: bfloat16 [2, 14336, 4096], P('section', 'col', 'row'), may hold values from -0.046875 to 0.046875
Outputs:
- input_grads: bfloat16 [2, 2, 48, 4096], P('section', None, 'col', 'row')
- grad_gate: float32 [2, 4096, 14336], P('section', 'row', 'col')
- grad_up: float32 [2, 4096, 14336], P('section', 'row', 'col')
- grad_down: float32 [2, 14336, 4096], P('section', 'col', 'row')
All inputs are finite; a program needn't handle non-finite values.
Results may differ from a plain program's by a relative error of at most 0.025.
Values may be sent and summed in bfloat16 or wider, within the bound.
A program may use at most 192 MiB of HBM per device.

v0:
```python
import jax
import jax.numpy as jnp
from jax import lax
from jax.experimental import pallas as pl
from jax.experimental.pallas import tpu as pltpu
from jax.sharding import PartitionSpec as P

CONTRACT_ROWS = (((0,), (0,)), ((), ()))
CONTRACT_COLS = (((1,), (1,)), ((), ()))


def passed_along(block, axis, distance):
    devices = range(lax.axis_size(axis))
    route = [(i - distance, i) for i in devices if i - distance in devices]
    return lax.ppermute(block, axis, route)


def spread_panel(panel):
    return lax.all_gather(panel, "col", axis=0, tiled=True)


def row_partials(make_terms, keep_rows):
    return lax.psum_scatter(
        make_terms(jnp.int32(0), keep_rows * lax.axis_size("row")).astype(jnp.bfloat16),
        "row",
        scatter_dimension=0,
        tiled=True,
    ).astype(jnp.float32)


def layer_backward(x_local, dy_local, w_both, w_down):
    hidden_width = w_down.shape[0]
    x_whole = spread_panel(x_local)
    dy_whole = spread_panel(dy_local)
    keep_rows = x_whole.shape[0] // lax.axis_size("row")

    def forward_terms(first_row, row_count):
        return jnp.dot(x_whole, w_both, preferred_element_type=jnp.float32)

    def backward_terms(first_row, row_count):
        return lax.dot_general(dy_whole, w_down, CONTRACT_COLS, preferred_element_type=jnp.float32)

    both_sums = row_partials(forward_terms, keep_rows)
    hidden_grad = row_partials(backward_terms, keep_rows)
    gate_sum = both_sums[:, :hidden_width]
    up_sum = both_sums[:, hidden_width:]
    sigmoid_gate = jax.nn.sigmoid(gate_sum)
    activated = gate_sum * sigmoid_gate
    slope = sigmoid_gate * (1.0 + gate_sum * (1.0 - sigmoid_gate))
    hidden = (activated * up_sum).astype(jnp.bfloat16)
    gate_grad = (hidden_grad * up_sum * slope).astype(jnp.bfloat16)
    up_grad = (hidden_grad * activated).astype(jnp.bfloat16)
    packed = jnp.concatenate([hidden, gate_grad, up_grad], axis=1)
    gathered = lax.all_gather(packed, "row", axis=0, tiled=True)
    hidden_whole = gathered[:, :hidden_width]
    both_grads = gathered[:, hidden_width:]
    branch_sum = lax.psum_scatter(
        lax.dot_general(
            both_grads, w_both, CONTRACT_COLS, preferred_element_type=jnp.float32
        ).astype(jnp.bfloat16),
        "col",
        scatter_dimension=0,
        tiled=True,
    ).astype(jnp.float32)
    input_grad = (dy_local.astype(jnp.float32) + branch_sum).astype(jnp.bfloat16)
    down_update = lax.dot_general(
        hidden_whole, dy_whole, CONTRACT_ROWS, preferred_element_type=jnp.float32
    )
    both_update = lax.dot_general(
        x_whole, both_grads, CONTRACT_ROWS, preferred_element_type=jnp.float32
    )
    return (input_grad, both_update, down_update)


def shards(section_inputs, out_grad, gate_weight, up_weight, down_weight):
    section_id = lax.axis_index("section")
    last_section = lax.axis_size("section") - 1
    is_last = section_id == last_section
    panels = section_inputs[0]
    w_both = jnp.concatenate([gate_weight[0], up_weight[0]], axis=1)
    w_down = down_weight[0]
    hidden_width = w_down.shape[0]
    micro_count = panels.shape[0]
    both_total = jnp.zeros(w_both.shape, jnp.float32)
    down_total = jnp.zeros(w_down.shape, jnp.float32)
    merged_shape = (micro_count * panels.shape[1], panels.shape[2])
    x_local = panels.reshape(merged_shape)
    top_grads = out_grad.reshape(merged_shape)
    received = jnp.zeros(merged_shape, jnp.bfloat16)
    merged_results = received
    for step_index in range(last_section + 1):
        is_active = section_id == last_section - step_index
        dy_local = jnp.where(is_last, top_grads, received)
        input_grad, both_update, down_update = layer_backward(x_local, dy_local, w_both, w_down)
        merged_results = jnp.where(is_active, input_grad, merged_results)
        both_total = both_total + jnp.where(is_active, both_update, 0.0)
        down_total = down_total + jnp.where(is_active, down_update, 0.0)
        if step_index < last_section:
            received = passed_along(input_grad, "section", -1)
    results = merged_results.reshape(panels.shape)
    return (
        results[None],
        both_total[:, :hidden_width][None],
        both_total[:, hidden_width:][None],
        down_total[None],
    )


ORDER = pl.DeviceIdType.MESH


def remote(src, dst, send_sem, recv_sem, target):
    return pltpu.make_async_remote_copy(
        src_ref=src, dst_ref=dst, send_sem=send_sem, recv_sem=recv_sem, device_id=target, device_id_type=ORDER
    )


def relay_kernel(
    x_ref, top_ref, gate_ref, up_ref, down_ref,
    grad_out, x_out, dy_out, packed_out,
    w_gate, w_up, w_down, x_slots, dy_slots, part_send, part_recv, spread, gate_sum, up_sum,
    branch, branch_send, branch_recv, result,
    w_sem, x_send_sem, x_recv_sem, dy_send_sem, dy_recv_sem, part_send_sem, part_recv_sem,
    spread_send_sem, spread_recv_sem, branch_send_sem, branch_recv_sem, onward_send_sem, onward_recv_sem, out_sem, go_sem,
):
    section = lax.axis_index("section")
    row = lax.axis_index("row")
    col = lax.axis_index("col")
    rows, width = part_send.shape[2], part_send.shape[3]
    local, micro = x_slots.shape[1:3]
    group = local * micro
    is_top = section == 1
    is_bottom = section == 0

    def row_peer(d):
        hi, lo = row // 2, row % 2
        return ((hi + d // 2) % 2) * 2 + (lo + d % 2) % 2

    def ahead(d):
        return (col + d) % 4

    def behind(d):
        return (col + 4 - d) % 4

    def weight_copy(a, d):
        cols = pl.ds(pl.multiple_of(row_peer(d) * width, width), width)
        if a == 2:
            return pltpu.make_async_copy(down_ref.at[cols, :], w_down.at[d], w_sem.at[2, d])
        source, target = ((gate_ref, w_gate), (up_ref, w_up))[a]
        return pltpu.make_async_copy(source.at[:, cols], target.at[d], w_sem.at[a, d])

    def x_copy(d):
        return remote(x_ref, x_slots.at[d], x_send_sem.at[d], x_recv_sem.at[d], (section, row, ahead(d)))

    def dy_copy(d):
        return remote(top_ref, dy_slots.at[d], dy_send_sem.at[d], dy_recv_sem.at[d], (section, row, ahead(d)))

    def pass_copy(d):
        return remote(result, dy_slots.at[d], dy_send_sem.at[d], dy_recv_sem.at[d], (0, row, ahead(d)))

    def half(h):
        return pl.ds(h * (rows // 2), rows // 2)

    def part_copy(a, d, h):
        return remote(
            part_send.at[a, d, half(h), :], part_recv.at[a, d, half(h), :],
            part_send_sem.at[a, d, h], part_recv_sem.at[a, d, h], (section, row_peer(d), col),
        )

    def spread_copy(a, d, h):
        return remote(
            spread.at[a, 0, half(h), :], spread.at[a, d, half(h), :],
            spread_send_sem.at[a, d, h], spread_recv_sem.at[a, d, h], (section, row_peer(d), col),
        )

    def onward_copy(a, d):
        return remote(
            spread.at[a, d, half(d - 1), :], spread.at[a, 3, half(d - 1), :],
            onward_send_sem.at[a, d], onward_recv_sem.at[a, d], (section, row_peer(3 - d), col),
        )

    def relay(*arrays):
        for d in (1, 2):
            for a in arrays:
                spread_copy(a, d, d - 1).wait_recv()
                onward_copy(a, d).start()
        for d in (1, 2):
            for a in arrays:
                spread_copy(a, d, 2 - d).wait_recv()

    def branch_copy(d):
        return remote(
            branch_send.at[d], branch_recv.at[d], branch_send_sem.at[d], branch_recv_sem.at[d],
            (section, row, behind(d)),
        )

    def merge(slots, whole):
        for d in range(4):
            for t in range(local):
                first = d * group + t * micro
                branch[first:first + micro, :] = slots[d, t].astype(jnp.float32)
        whole[...] = branch[...].astype(jnp.bfloat16)

    for d in (3, 2, 1, 0):
        weight_copy(0, d).start()
        weight_copy(1, d).start()
    for d in (3, 2, 1, 0):
        weight_copy(2, d).start()

    barrier = pltpu.get_barrier_semaphore()
    greeted = [(section, row, ahead(d)) for d in (1, 2, 3)]
    greeted += [(section, row_peer(d), col) for d in (1, 2, 3)]
    greeted += [(1 - section, row, ahead(d)) for d in range(4)]
    for device in greeted:
        pl.semaphore_signal(barrier, inc=1, device_id=device, device_id_type=ORDER)
    pl.semaphore_wait(barrier, len(greeted))

    for d in (2, 1, 3):
        x_copy(d).start()
    x_slots[0] = x_ref[...]

    @pl.when(is_top)
    def _():
        for d in (2, 1, 3):
            dy_copy(d).start()
        dy_slots[0] = top_ref[...]

    def hidden_terms():
        merge(dy_slots, dy_out)

        def step(i, carry):
            d = 3 - i
            weight_copy(2, d).wait()
            part_send[2, d] = lax.dot_general(
                dy_out[...], w_down[d], CONTRACT_COLS, preferred_element_type=jnp.float32
            ).astype(jnp.bfloat16)

            @pl.when(d > 0)
            def _():
                part_copy(2, d, 0).start()
            return carry

        lax.fori_loop(0, 4, step, 0)

    for d in (1, 2, 3):
        x_copy(d).wait_recv()
    merge(x_slots, x_out)

    def forward_step(i, carry):
        d = 3 - i
        weight_copy(0, d).wait()
        weight_copy(1, d).wait()
        for a, weight in enumerate((w_gate, w_up)):
            part_send[a, d] = jnp.dot(
                x_out[...], weight[d], preferred_element_type=jnp.float32
            ).astype(jnp.bfloat16)

            @pl.when(jnp.logical_and(is_top, d > 0))
            def _():
                part_copy(a, d, 0).start()
        return carry

    lax.fori_loop(0, 4, forward_step, 0)

    @pl.when(is_bottom)
    def _():
        pl.semaphore_wait(go_sem, 1)
        for h in range(2):
            for d in (3, 2, 1):
                for a in range(2):
                    part_copy(a, d, h).start()
        for d in range(4):
            pass_copy(d).wait_recv()

    @pl.when(is_top)
    def _():
        for d in (1, 2, 3):
            dy_copy(d).wait_recv()

    hidden_terms()

    @pl.when(is_top)
    def _():
        for d in (3, 2, 1):
            for a in range(2):
                part_copy(a, d, 1).start()

    for d in (3, 2, 1):
        part_copy(2, d, 1).start()

    def summed(a, span):
        total = part_send[a, 0, span, :].astype(jnp.float32)
        for d in (1, 2, 3):
            total = total + part_recv[a, d, span, :].astype(jnp.float32)
        return total

    def span_of(i):
        return pl.ds(pl.multiple_of(i * 16, 16), 16)

    def hidden_step(i, carry):
        span = span_of(i)
        gate, up = summed(0, span), summed(1, span)
        gate_sum[span, :] = gate
        up_sum[span, :] = up
        spread[0, 0, span, :] = (gate * jax.nn.sigmoid(gate) * up).astype(jnp.bfloat16)
        return carry

    def grad_step(i, carry):
        span = span_of(i)
        hidden_grad = summed(2, span)
        gate, up = gate_sum[span, :], up_sum[span, :]
        sigmoid_gate = jax.nn.sigmoid(gate)
        slope = sigmoid_gate * (1.0 + gate * (1.0 - sigmoid_gate))
        spread[1, 0, span, :] = (hidden_grad * up * slope).astype(jnp.bfloat16)
        spread[2, 0, span, :] = (hidden_grad * (gate * sigmoid_gate)).astype(jnp.bfloat16)
        return carry

    steps = rows // 32
    for h in range(2):
        for a in range(2):
            for d in (1, 2, 3):
                part_copy(a, d, h).wait_recv()
        lax.fori_loop(h * steps, (h + 1) * steps, hidden_step, 0)
        for d in (1, 2, 3):
            part_copy(2, d, h).wait_recv()
        lax.fori_loop(h * steps, (h + 1) * steps, grad_step, 0)
        for a in (1, 2):
            for d in (1, 2):
                spread_copy(a, d, h).start()

    @pl.when(is_bottom)
    def _():
        for h in range(2):
            for d in (1, 2):
                spread_copy(0, d, h).start()

    def partner_go():
        pl.semaphore_signal(go_sem, inc=1, device_id=(1 - section, row, col), device_id_type=ORDER)

    branch[...] = jnp.zeros_like(branch)

    def branch_step(d, carry):
        @pl.when(d == 1)
        def _():
            relay(1, 2)

        @pl.when(d == 3)
        def _():
            for a in (1, 2):
                for e in (1, 2):
                    onward_copy(a, e).wait_recv()
            partner_go()

        branch[...] += lax.dot_general(
            spread[1, d], w_gate[d], CONTRACT_COLS, preferred_element_type=jnp.float32
        ) + lax.dot_general(
            spread[2, d], w_up[d], CONTRACT_COLS, preferred_element_type=jnp.float32
        )
        return carry

    lax.fori_loop(0, 4, branch_step, 0)
    for d in (2, 3, 1, 0):
        branch_send[d] = branch[d * group:(d + 1) * group, :].astype(jnp.bfloat16)
        if d:
            branch_copy(d).start()

    def store_copy(a, d):
        cols = pl.ds(pl.multiple_of(row_peer(d) * width, width), width)
        return pltpu.make_async_copy(spread.at[a, d], packed_out.at[a, :, cols], out_sem.at[a, d])

    for a in (1, 2):
        for d in range(4):
            store_copy(a, d).start()

    total = dy_out[:group, :].astype(jnp.float32) + branch_send[0].astype(jnp.float32)
    for d in (1, 2, 3):
        branch_copy(d).wait_recv()
        total = total + branch_recv[d].astype(jnp.float32)
    branch[:group, :] = total
    for t in range(local):
        result[t] = branch[t * micro:(t + 1) * micro, :].astype(jnp.bfloat16)

    @pl.when(is_top)
    def _():
        for d in (2, 1, 3, 0):
            pass_copy(d).start()
        pl.semaphore_wait(go_sem, 1)
        for h in range(2):
            for d in (1, 2):
                spread_copy(0, d, h).start()

    grad_out[...] = result[...]
    relay(0)
    for d in (1, 2):
        onward_copy(0, d).wait_recv()
    for d in range(4):
        store_copy(0, d).start()
    for a in range(3):
        for d in range(4):
            store_copy(a, d).wait()
    for d in (1, 2, 3):
        x_copy(d).wait_send()
        branch_copy(d).wait_send()
        for a in range(3):
            for h in range(2):
                part_copy(a, d, h).wait_send()
    for d in (1, 2):
        for a in range(3):
            for h in range(2):
                spread_copy(a, d, h).wait_send()
            onward_copy(a, d).wait_send()

    @pl.when(is_top)
    def _():
        for d in (1, 2, 3):
            dy_copy(d).wait_send()
        for d in range(4):
            pass_copy(d).wait_send()


def update_kernel(x_ref, dy_ref, packed_ref, gate_out, up_out, down_out):
    for left, right, out in (
        (x_ref[...], packed_ref[1], gate_out),
        (x_ref[...], packed_ref[2], up_out),
        (packed_ref[0], dy_ref[...], down_out),
    ):
        out[...] = lax.dot_general(left, right, CONTRACT_ROWS, preferred_element_type=jnp.float32)


def weight_updates(x_whole, dy_whole, packed):
    rows, width = x_whole.shape
    hidden_width = packed.shape[2]
    tile = next(t for t in (512, 256, 128) if hidden_width % t == 0)
    f32 = jnp.float32
    whole = pl.BlockSpec((rows, width), lambda j: (0, 0))
    wide = pl.BlockSpec((width, tile), lambda j: (0, j))
    return pl.pallas_call(
        update_kernel,
        grid=(hidden_width // tile,),
        out_shape=(
            jax.ShapeDtypeStruct((width, hidden_width), f32),
            jax.ShapeDtypeStruct((width, hidden_width), f32),
            jax.ShapeDtypeStruct((hidden_width, width), f32),
        ),
        in_specs=[whole, whole, pl.BlockSpec((3, rows, tile), lambda j: (0, 0, j))],
        out_specs=(wide, wide, pl.BlockSpec((tile, width), lambda j: (j, 0))),
        compiler_params=pltpu.CompilerParams(vmem_limit_bytes=60 * 2**20),
    )(x_whole, dy_whole, packed)


def fast_shards(section_inputs, out_grad, gate_weight, up_weight, down_weight):
    panels = section_inputs[0]
    micro, local, width = panels.shape
    group = micro * local
    held = (local, micro, width)
    rows = group * lax.axis_size("col")
    hidden_width = gate_weight.shape[2]
    piece = hidden_width // lax.axis_size("row")
    vmem = pl.BlockSpec(memory_space=pltpu.VMEM)
    anywhere = pl.BlockSpec(memory_space=pl.ANY)
    bf16, f32 = jnp.bfloat16, jnp.float32
    dma = pltpu.SemaphoreType.DMA
    grad, x_whole, dy_whole, packed = pl.pallas_call(
        relay_kernel,
        out_shape=(
            jax.ShapeDtypeStruct(held, bf16),
            jax.ShapeDtypeStruct((rows, width), bf16),
            jax.ShapeDtypeStruct((rows, width), bf16),
            jax.ShapeDtypeStruct((3, rows, hidden_width), bf16),
        ),
        in_specs=[vmem, vmem, anywhere, anywhere, anywhere],
        out_specs=(vmem, vmem, vmem, anywhere),
        scratch_shapes=[
            pltpu.VMEM((4, width, piece), bf16),
            pltpu.VMEM((4, width, piece), bf16),
            pltpu.VMEM((4, piece, width), bf16),
            pltpu.VMEM((4, *held), bf16),
            pltpu.VMEM((4, *held), bf16),
            pltpu.VMEM((3, 4, rows, piece), bf16),
            pltpu.VMEM((3, 4, rows, piece), bf16),
            pltpu.VMEM((3, 4, rows, piece), bf16),
            pltpu.VMEM((rows, piece), f32),
            pltpu.VMEM((rows, piece), f32),
            pltpu.VMEM((rows, width), f32),
            pltpu.VMEM((4, group, width), bf16),
            pltpu.VMEM((4, group, width), bf16),
            pltpu.VMEM(held, bf16),
            dma((3, 4)), dma((4,)), dma((4,)), dma((4,)), dma((4,)),
            *[dma((3, 4, 2))] * 4, dma((4,)), dma((4,)),
            dma((3, 4)), dma((3, 4)), dma((3, 4)), pltpu.SemaphoreType.REGULAR,
        ],
        compiler_params=pltpu.CompilerParams(collective_id=0, has_side_effects=True, vmem_limit_bytes=56 * 2**20),
    )(
        panels.transpose(1, 0, 2), out_grad.transpose(1, 0, 2),
        gate_weight[0], up_weight[0], down_weight[0],
    )
    grads = weight_updates(x_whole, dy_whole, packed)
    grad = grad.transpose(1, 0, 2)
    return (grad[None], *(g[None] for g in grads))


def fits_kernel(mesh, gate_weight, section_inputs):
    sizes = mesh.shape
    if (sizes["section"], sizes["row"], sizes["col"]) != (2, 4, 4):
        return False
    piece = gate_weight.shape[2] // (sizes["row"] * sizes["col"])
    local = section_inputs.shape[1] * section_inputs.shape[2] // sizes["col"]
    return piece % 128 == 0 and local % 8 == 0 and (local * sizes["col"]) % 32 == 0


def solution(mesh):
    specs = dict(
        mesh=mesh,
        in_specs=(
            P("section", None, "col", "row"),
            P(None, "col", "row"),
            P("section", "row", "col"),
            P("section", "row", "col"),
            P("section", "col", "row"),
        ),
        out_specs=(
            P("section", None, "col", "row"),
            P("section", "row", "col"),
            P("section", "row", "col"),
            P("section", "col", "row"),
        ),
        check_vma=False,
    )

    def run(section_inputs, out_grad, gate_weight, up_weight, down_weight):
        body = fast_shards if fits_kernel(mesh, gate_weight, section_inputs) else shards
        return jax.shard_map(body, **specs)(section_inputs, out_grad, gate_weight, up_weight, down_weight)

    return run
```

profile of v0, /device:TPU:0, one launch (start us, length us, event | category | flops | bytes accessed | tf_op | source)
XLA Modules:
  0.0 88.1 jit_solution(9547949476206491494)
XLA Ops:
  0.6 70.3 %shard_map.84 = (bf16[12,2,1024]{2,1,0:T(2,128)(2,1)}, bf16[96,1024]{1,0:T(8,128)(2,1)}, bf16[96,1024]{1,0:T(8,128)(2,1)}, bf16[3,96,3584]{2,1,0:T(8,128)(2,1)}) custom-call(bf16[12,2,1024]{2,1,0:T(2,128)(2,1)} %bitcast.17, bf16[12,2,1024]{2,1,0:T(2,128)(2,1)} %bitcast.18, bf16[1024,3584]{1,0:T(8,128)(2,1)} %bitcast.13, bf16[1024,3584]{1,0:T(8,128)(2,1)} %bitcast.14, ...), custom_call_target="tpu_custom_call" | custom-call | tf_op jit(solution)/shard_map/pallas_call | solution.py:463
  71.0 15.6 %shard_map.85 = (f32[1024,3584]{1,0:T(8,128)}, f32[1024,3584]{1,0:T(8,128)}, f32[3584,1024]{1,0:T(8,128)}) custom-call(bf16[96,1024]{1,0:T(8,128)(2,1)} %get-tuple-element.12.x_ref, bf16[96,1024]{1,0:T(8,128)(2,1)} %get-tuple-element.13.dy_ref, bf16[3,96,3584]{2,1,0:T(8,128)(2,1)} %get-tuple-element.14.packed_ref), custom_call_target="tpu_custom_call" | custom-call | tf_op jit(solution)/shard_map/pallas_call | solution.py:437
  86.6 1.5 %copy.10 = bf16[1,2,12,1024]{3,1,2,0:T(2,128)(2,1)} copy(bf16[1,2,12,1024]{3,1,2,0:T(2,128)(2,1)} %bitcast.16) | data formatting | bytes 98304
where the time goes:
time: 88.3 us; the launch traced here: 88.1 us
  Pallas kernels  86 us (97%)
  local copies, waits for them, and re-layouts  1.45 us (2%)
    pallas_call x1, Pallas kernels, fast_shards(): pl.pallas_call(relay_kernel, out_shape=(jax.ShapeDtypeStruct(held, bf16),...  70.3 us
    pallas_call x1, Pallas kernels, weight_updates(): pl.pallas_call(update_kernel, grid=(hidden_width // tile,), out_shape=(ja...  15.6 us

commit v1 on v0

v1 whole, which is shorter than its diff:
```python
import jax
import jax.numpy as jnp
from jax import lax
from jax.experimental import pallas as pl
from jax.experimental.pallas import tpu as pltpu
from jax.sharding import PartitionSpec as P

CONTRACT_ROWS = (((0,), (0,)), ((), ()))
CONTRACT_COLS = (((1,), (1,)), ((), ()))


def passed_along(block, axis, distance):
    devices = range(lax.axis_size(axis))
    route = [(i - distance, i) for i in devices if i - distance in devices]
    return lax.ppermute(block, axis, route)


def spread_panel(panel):
    return lax.all_gather(panel, "col", axis=0, tiled=True)


def row_partials(make_terms, keep_rows):
    return lax.psum_scatter(
        make_terms(jnp.int32(0), keep_rows * lax.axis_size("row")).astype(jnp.bfloat16),
        "row",
        scatter_dimension=0,
        tiled=True,
    ).astype(jnp.float32)


def layer_backward(x_local, dy_local, w_both, w_down):
    hidden_width = w_down.shape[0]
    x_whole = spread_panel(x_local)
    dy_whole = spread_panel(dy_local)
    keep_rows = x_whole.shape[0] // lax.axis_size("row")

    def forward_terms(first_row, row_count):
        return jnp.dot(x_whole, w_both, preferred_element_type=jnp.float32)

    def backward_terms(first_row, row_count):
        return lax.dot_general(dy_whole, w_down, CONTRACT_COLS, preferred_element_type=jnp.float32)

    both_sums = row_partials(forward_terms, keep_rows)
    hidden_grad = row_partials(backward_terms, keep_rows)
    gate_sum = both_sums[:, :hidden_width]
    up_sum = both_sums[:, hidden_width:]
    sigmoid_gate = jax.nn.sigmoid(gate_sum)
    activated = gate_sum * sigmoid_gate
    slope = sigmoid_gate * (1.0 + gate_sum * (1.0 - sigmoid_gate))
    hidden = (activated * up_sum).astype(jnp.bfloat16)
    gate_grad = (hidden_grad * up_sum * slope).astype(jnp.bfloat16)
    up_grad = (hidden_grad * activated).astype(jnp.bfloat16)
    packed = jnp.concatenate([hidden, gate_grad, up_grad], axis=1)
    gathered = lax.all_gather(packed, "row", axis=0, tiled=True)
    hidden_whole = gathered[:, :hidden_width]
    both_grads = gathered[:, hidden_width:]
    branch_sum = lax.psum_scatter(
        lax.dot_general(
            both_grads, w_both, CONTRACT_COLS, preferred_element_type=jnp.float32
        ).astype(jnp.bfloat16),
        "col",
        scatter_dimension=0,
        tiled=True,
    ).astype(jnp.float32)
    input_grad = (dy_local.astype(jnp.float32) + branch_sum).astype(jnp.bfloat16)
    down_update = lax.dot_general(
        hidden_whole, dy_whole, CONTRACT_ROWS, preferred_element_type=jnp.float32
    )
    both_update = lax.dot_general(
        x_whole, both_grads, CONTRACT_ROWS, preferred_element_type=jnp.float32
    )
    return (input_grad, both_update, down_update)


def shards(section_inputs, out_grad, gate_weight, up_weight, down_weight):
    section_id = lax.axis_index("section")
    last_section = lax.axis_size("section") - 1
    is_last = section_id == last_section
    panels = section_inputs[0]
    w_both = jnp.concatenate([gate_weight[0], up_weight[0]], axis=1)
    w_down = down_weight[0]
    hidden_width = w_down.shape[0]
    micro_count = panels.shape[0]
    both_total = jnp.zeros(w_both.shape, jnp.float32)
    down_total = jnp.zeros(w_down.shape, jnp.float32)
    merged_shape = (micro_count * panels.shape[1], panels.shape[2])
    x_local = panels.reshape(merged_shape)
    top_grads = out_grad.reshape(merged_shape)
    received = jnp.zeros(merged_shape, jnp.bfloat16)
    merged_results = received
    for step_index in range(last_section + 1):
        is_active = section_id == last_section - step_index
        dy_local = jnp.where(is_last, top_grads, received)
        input_grad, both_update, down_update = layer_backward(x_local, dy_local, w_both, w_down)
        merged_results = jnp.where(is_active, input_grad, merged_results)
        both_total = both_total + jnp.where(is_active, both_update, 0.0)
        down_total = down_total + jnp.where(is_active, down_update, 0.0)
        if step_index < last_section:
            received = passed_along(input_grad, "section", -1)
    results = merged_results.reshape(panels.shape)
    return (
        results[None],
        both_total[:, :hidden_width][None],
        both_total[:, hidden_width:][None],
        down_total[None],
    )


ORDER = pl.DeviceIdType.MESH


def remote(src, dst, send_sem, recv_sem, target):
    return pltpu.make_async_remote_copy(
        src_ref=src, dst_ref=dst, send_sem=send_sem, recv_sem=recv_sem, device_id=target, device_id_type=ORDER
    )


def relay_kernel(
    x_ref, top_ref, gate_ref, up_ref, down_ref,
    grad_out, x_out, dy_out, packed_out,
    w_gate, w_up, w_down, x_slots, dy_slots, x_whole, dy_whole, stage, part_send, part_recv, spread, gate_sum, up_sum, terms,
    branch, branch_send, branch_recv, result,
    w_sem, in_sem, x_send_sem, x_recv_sem, dy_send_sem, dy_recv_sem, part_send_sem, part_recv_sem,
    spread_send_sem, spread_recv_sem, onward_send_sem, onward_recv_sem, branch_send_sem, branch_recv_sem, out_sem, last_sem,
    go_sem,
):
    section = lax.axis_index("section")
    row = lax.axis_index("row")
    col = lax.axis_index("col")
    rows, width = part_send.shape[2], part_send.shape[3]
    local, micro = x_slots.shape[1:3]
    span = rows // 2
    group = local * micro
    block = x_slots.shape[3] // 2
    is_top = section == 1
    is_bottom = section == 0

    def row_peer(d):
        hi, lo = row // 2, row % 2
        return ((hi + d // 2) % 2) * 2 + (lo + d % 2) % 2

    def ahead(d):
        return (col + d) % 4

    def behind(d):
        return (col + 4 - d) % 4

    def half(h):
        return pl.ds(h * span, span)

    def block_of(c):
        return pl.ds(pl.multiple_of(c * block, block), block)

    def weight_copy(a, d):
        cols = pl.ds(pl.multiple_of(row_peer(d) * width, width), width)
        if a == 2:
            return pltpu.make_async_copy(down_ref.at[cols, :], w_down.at[d], w_sem.at[2, d])
        source, target = ((gate_ref, w_gate), (up_ref, w_up))[a]
        return pltpu.make_async_copy(source.at[:, cols], target.at[d], w_sem.at[a, d])

    def x_copy(d):
        return remote(x_slots.at[0], x_slots.at[d], x_send_sem.at[d], x_recv_sem.at[d], (section, row, ahead(d)))

    def dy_copy(d, c):
        return remote(
            dy_slots.at[c, 0], dy_slots.at[c, d], dy_send_sem.at[d, c], dy_recv_sem.at[d, c], (section, row, ahead(d))
        )

    def pass_copy(d, c):
        return remote(
            result.at[c], dy_slots.at[c, d], dy_send_sem.at[d, c], dy_recv_sem.at[d, c], (0, row, ahead(d))
        )

    def part_copy(a, d, h):
        place = (a, d, half(h), slice(None))
        via = (d - 2 * (d // 3), d - d // 3, d)[a]
        return remote(
            part_send.at[place], part_recv.at[place],
            part_send_sem.at[a, d, h], part_recv_sem.at[a, d, h], (section, row_peer(via), col),
        )

    def relay_sum(a, h):
        middle = 2 - a
        part_copy(a, 3, h).wait_recv()
        total = part_send[a, middle, half(h), :].astype(jnp.float32) + part_recv[a, 3, half(h), :].astype(jnp.float32)
        part_send[a, middle, half(h), :] = total.astype(jnp.bfloat16)
        part_copy(a, middle, h).start()

    def spread_copy(a, d, h):
        return remote(
            spread.at[a, 0, half(h), :], spread.at[a, d, half(h), :],
            spread_send_sem.at[a, d, h], spread_recv_sem.at[a, d, h], (section, row_peer(d), col),
        )

    def onward_copy(a, h):
        d = (1 + h, 1, 2)[a]
        return remote(
            spread.at[a, d, half(h), :], spread.at[a, 3, half(h), :],
            onward_send_sem.at[a, h], onward_recv_sem.at[a, h], (section, row_peer(3 - d), col),
        )

    def spread_grads(h):
        for a, d in ((1, 1), (2, 2), (2, 1), (1, 2)):
            spread_copy(a, d, h).start()

    def relay_grads(h):
        for a in (1, 2):
            spread_copy(a, a, h).wait_recv()
            onward_copy(a, h).start()

    def spread_hidden():
        for h, d in ((0, 1), (1, 2), (1, 1), (0, 2)):
            spread_copy(0, d, h).start()

    def relay_hidden():
        for h in range(2):
            spread_copy(0, 1 + h, h).wait_recv()
            onward_copy(0, h).start()

    def branch_copy(d, c):
        return remote(
            branch_send.at[c, d], branch_recv.at[c, d], branch_send_sem.at[d, c], branch_recv_sem.at[d, c],
            (section, row, behind(d)),
        )

    def store_copy(a, d):
        cols = pl.ds(pl.multiple_of(row_peer(d) * width, width), width)
        return pltpu.make_async_copy(spread.at[a, d], packed_out.at[a, :, cols], out_sem.at[a, d])

    def last_copy(which, c):
        source, target = (
            (x_whole.at[:, block_of(c)], x_out.at[:, block_of(c)]),
            (dy_whole.at[c], dy_out.at[:, block_of(c)]),
            (result.at[c], grad_out.at[:, :, block_of(c)]),
        )[which]
        return pltpu.make_async_copy(source, target, last_sem.at[which, c])

    def merge(slots, arrive):
        for d in range(4):
            arrive(d)
            for t in range(local):
                first = d * group + t * micro
                stage[first:first + micro, :slots.shape[3]] = slots[d, t].astype(jnp.float32)

    def merge_dy(c, arrive):
        merge(dy_slots.at[c], arrive)
        dy_whole[c] = stage[:, :block].astype(jnp.bfloat16)
        last_copy(1, c).start()

    x_load = pltpu.make_async_copy(x_ref, x_slots.at[0], in_sem.at[0])

    def top_load(c):
        return pltpu.make_async_copy(top_ref.at[:, :, block_of(c)], dy_slots.at[c, 0], in_sem.at[1 + c])

    x_load.start()

    @pl.when(is_top)
    def _():
        for c in range(2):
            top_load(c).start()

    barrier = pltpu.get_barrier_semaphore()
    greeted = [(section, row, ahead(d)) for d in (1, 2, 3)]
    greeted += [(section, row_peer(d), col) for d in (1, 2, 3)]
    greeted += [(1 - section, row, ahead(d)) for d in range(4)]
    for device in greeted:
        pl.semaphore_signal(barrier, inc=1, device_id=device, device_id_type=ORDER)
    x_load.wait()

    @pl.when(is_top)
    def _():
        for c in range(2):
            top_load(c).wait()

    for d in (3, 2, 1, 0):
        weight_copy(0, d).start()
        weight_copy(1, d).start()
    for d in (3, 2, 1, 0):
        weight_copy(2, d).start()

    pl.semaphore_wait(barrier, len(greeted))

    def partner_go(which):
        pl.semaphore_signal(
            go_sem.at[which], inc=1, device_id=(1 - section, row, col), device_id_type=ORDER
        )

    @pl.when(is_bottom)
    def _():
        pl.semaphore_wait(go_sem.at[0], 1)

    for d in (2, 1, 3):
        x_copy(d).start()

    @pl.when(is_top)
    def _():
        for c in range(2):
            for d in (2, 1, 3):
                dy_copy(d, c).start()

    def x_arrive(d):
        if d:
            x_copy(d).wait_recv()

    merge(x_slots, x_arrive)

    @pl.when(is_top)
    def _():
        partner_go(0)

    x_whole[...] = stage[...].astype(jnp.bfloat16)
    for c in range(2):
        last_copy(0, c).start()

    def forward_step(i, carry):
        d = 3 - i
        weight_copy(0, d).wait()
        weight_copy(1, d).wait()
        for a, weight in enumerate((w_gate, w_up)):
            part_send[a, d] = jnp.dot(
                x_whole[...], weight[d], preferred_element_type=jnp.float32
            ).astype(jnp.bfloat16)

            @pl.when(jnp.logical_and(is_top, (d % 2 == 1, d >= 2)[a]))
            def _():
                for h in range(2):
                    part_copy(a, d, h).start()
        return carry

    lax.fori_loop(0, 4, forward_step, 0)

    def summed(a, where):
        total = part_send[a, 0, where, :].astype(jnp.float32)
        for d in range(1, 4 if a == 2 else 3):
            total = total + part_recv[a, d, where, :].astype(jnp.float32)
        return total

    def rows_of(i):
        return pl.ds(pl.multiple_of(i * 16, 16), 16)

    def hidden_step(i, carry):
        where = rows_of(i)
        gate, up = summed(0, where), summed(1, where)
        gate_sum[where, :] = gate
        up_sum[where, :] = up
        spread[0, 0, where, :] = (gate * jax.nn.sigmoid(gate) * up).astype(jnp.bfloat16)
        return carry

    def grad_step(i, carry):
        where = rows_of(i)
        hidden_grad = summed(2, where)
        gate, up = gate_sum[where, :], up_sum[where, :]
        sigmoid_gate = jax.nn.sigmoid(gate)
        slope = sigmoid_gate * (1.0 + gate * (1.0 - sigmoid_gate))
        spread[1, 0, where, :] = (hidden_grad * up * slope).astype(jnp.bfloat16)
        spread[2, 0, where, :] = (hidden_grad * (gate * sigmoid_gate)).astype(jnp.bfloat16)
        return carry

    steps = span // 16

    def hidden_rows(h):
        for a in range(2):
            for d in (1, 2):
                part_copy(a, d, h).wait_recv()
        lax.fori_loop(h * steps, (h + 1) * steps, hidden_step, 0)

    def grad_rows(h):
        for d in (1, 2, 3):
            part_copy(2, d, h).wait_recv()
        lax.fori_loop(h * steps, (h + 1) * steps, grad_step, 0)
        spread_grads(h)

    @pl.when(is_bottom)
    def _():
        pl.semaphore_wait(go_sem.at[1], 1)
        for a, d in ((0, 3), (1, 3), (0, 1), (1, 2)):
            for h in range(2):
                part_copy(a, d, h).start()

    for a in range(2):
        relay_sum(a, 0)

    @pl.when(is_bottom)
    def _():
        for a in range(2):
            relay_sum(a, 1)
        for h in range(2):
            hidden_rows(h)
        spread_hidden()

    def merge_block(c):
        @pl.when(is_top)
        def _():
            merge_dy(c, lambda d: dy_copy(d, c).wait_recv() if d else None)

        @pl.when(is_bottom)
        def _():
            merge_dy(c, lambda d: pass_copy(d, c).wait_recv())

    def grad_terms_step(k, carry):
        c = section * (k % 2) + (1 - section) * (k // 4)
        d = 3 - section * (k // 2) - (1 - section) * (k % 4)

        @pl.when(k == 0)
        def _():
            merge_block(0)

        @pl.when(k == 4 - 3 * section)
        def _():
            merge_block(1)

        @pl.when(jnp.logical_and(is_top, k == 4))
        def _():
            for a in range(2):
                relay_sum(a, 1)

        @pl.when(c == 0)
        def _():
            weight_copy(2, d).wait()

        term = lax.dot_general(
            dy_whole[c], w_down[d, :, block_of(c)], CONTRACT_COLS, preferred_element_type=jnp.float32
        )

        @pl.when(c == 0)
        def _():
            terms[d] = term

        @pl.when(c == 1)
        def _():
            part_send[2, d] = (terms[d] + term).astype(jnp.bfloat16)

            @pl.when(d > 0)
            def _():
                part_copy(2, d, 0).start()
        return carry

    lax.fori_loop(0, 8, grad_terms_step, 0)
    for d in (3, 2, 1):
        part_copy(2, d, 1).start()

    @pl.when(is_top)
    def _():
        for h in range(2):
            hidden_rows(h)

    @pl.when(is_bottom)
    def _():
        relay_hidden()

    for h in range(2):
        grad_rows(h)

    def send_branch(c):
        for d in (2, 3, 1):
            first = d * group
            branch_send[c, d] = branch[c, first:first + group, :].astype(jnp.bfloat16)
            branch_copy(d, c).start()

    def branch_step(k, carry):
        d = k // 2
        c = k % 2

        @pl.when(k == 2)
        def _():
            for h in range(2):
                relay_grads(h)

            @pl.when(is_top)
            def _():
                partner_go(1)
                spread_hidden()

            for h in range(2):
                spread_copy(2, 1, h).wait_recv()

        @pl.when(k == 4)
        def _():
            for h in range(2):
                spread_copy(1, 2, h).wait_recv()

        @pl.when(k == 6)
        def _():
            for h in range(2):
                for a in (1, 2):
                    onward_copy(a, h).wait_recv()

        @pl.when(k == 7)
        def _():
            send_branch(0)

        term = lax.dot_general(
            spread[1, d], w_gate[d, block_of(c), :], CONTRACT_COLS, preferred_element_type=jnp.float32
        ) + lax.dot_general(
            spread[2, d], w_up[d, block_of(c), :], CONTRACT_COLS, preferred_element_type=jnp.float32
        )

        @pl.when(d == 0)
        def _():
            branch[c] = term

        @pl.when(d > 0)
        def _():
            branch[c] += term
        return carry

    lax.fori_loop(0, 8, branch_step, 0)
    send_branch(1)
    for a in (1, 2):
        for d in range(4):
            store_copy(a, d).start()

    for c in range(2):
        total = dy_whole[c, :group, :].astype(jnp.float32) + branch[c, :group, :]
        for d in (1, 2, 3):
            branch_copy(d, c).wait_recv()
            total = total + branch_recv[c, d].astype(jnp.float32)
        stage[:group, :block] = total
        for t in range(local):
            result[c, t] = stage[t * micro:(t + 1) * micro, :block].astype(jnp.bfloat16)

        @pl.when(is_top)
        def _():
            for d in (2, 3, 1, 0):
                pass_copy(d, c).start()

        last_copy(2, c).start()

    @pl.when(is_top)
    def _():
        relay_hidden()

    for h in range(2):
        spread_copy(0, 2 - h, h).wait_recv()
        onward_copy(0, h).wait_recv()
    for d in range(4):
        store_copy(0, d).start()
    for d in (1, 2, 3):
        x_copy(d).wait_send()
        for h in range(2):
            branch_copy(d, h).wait_send()
            for a in range(3):
                part_copy(a, d, h).wait_send()
    for h in range(2):
        for a in range(3):
            for d in (1, 2):
                spread_copy(a, d, h).wait_send()
            onward_copy(a, h).wait_send()

    @pl.when(is_top)
    def _():
        for h in range(2):
            for d in (1, 2, 3):
                dy_copy(d, h).wait_send()
            for d in range(4):
                pass_copy(d, h).wait_send()

    for a in range(3):
        for d in range(4):
            store_copy(a, d).wait()
    for which in range(3):
        for c in range(2):
            last_copy(which, c).wait()


def update_kernel(x_ref, dy_ref, packed_ref, gate_out, up_out, down_out):
    for left, right, out in (
        (x_ref[...], packed_ref[1], gate_out),
        (x_ref[...], packed_ref[2], up_out),
        (packed_ref[0], dy_ref[...], down_out),
    ):
        out[...] = lax.dot_general(left, right, CONTRACT_ROWS, preferred_element_type=jnp.float32)


def weight_updates(x_whole, dy_whole, packed):
    rows, width = x_whole.shape
    hidden_width = packed.shape[2]
    tile = next(t for t in (512, 256, 128) if hidden_width % t == 0)
    f32 = jnp.float32
    whole = pl.BlockSpec((rows, width), lambda j: (0, 0))
    wide = pl.BlockSpec((width, tile), lambda j: (0, j))
    return pl.pallas_call(
        update_kernel,
        grid=(hidden_width // tile,),
        out_shape=(
            jax.ShapeDtypeStruct((width, hidden_width), f32),
            jax.ShapeDtypeStruct((width, hidden_width), f32),
            jax.ShapeDtypeStruct((hidden_width, width), f32),
        ),
        in_specs=[whole, whole, pl.BlockSpec((3, rows, tile), lambda j: (0, 0, j))],
        out_specs=(wide, wide, pl.BlockSpec((tile, width), lambda j: (j, 0))),
        compiler_params=pltpu.CompilerParams(vmem_limit_bytes=60 * 2**20),
    )(x_whole, dy_whole, packed)


def fast_shards(section_inputs, out_grad, gate_weight, up_weight, down_weight):
    panels = section_inputs[0]
    micro, local, width = panels.shape
    group = micro * local
    held = (local, micro, width)
    rows = group * lax.axis_size("col")
    hidden_width = gate_weight.shape[2]
    piece = hidden_width // lax.axis_size("row")
    hbm = pl.BlockSpec(memory_space=pltpu.HBM)
    bf16, f32 = jnp.bfloat16, jnp.float32
    dma = pltpu.SemaphoreType.DMA
    block = width // 2
    grad, x_whole, dy_whole, packed = pl.pallas_call(
        relay_kernel,
        out_shape=(
            jax.ShapeDtypeStruct(held, bf16),
            jax.ShapeDtypeStruct((rows, width), bf16),
            jax.ShapeDtypeStruct((rows, width), bf16),
            jax.ShapeDtypeStruct((3, rows, hidden_width), bf16),
        ),
        in_specs=[hbm] * 5,
        out_specs=(hbm,) * 4,
        scratch_shapes=[
            pltpu.VMEM((4, width, piece), bf16),
            pltpu.VMEM((4, width, piece), bf16),
            pltpu.VMEM((4, piece, width), bf16),
            pltpu.VMEM((4, *held), bf16),
            pltpu.VMEM((2, 4, local, micro, block), bf16),
            pltpu.VMEM((rows, width), bf16),
            pltpu.VMEM((2, rows, block), bf16),
            pltpu.VMEM((rows, width), f32),
            pltpu.VMEM((3, 4, rows, piece), bf16),
            pltpu.VMEM((3, 4, rows, piece), bf16),
            pltpu.VMEM((3, 4, rows, piece), bf16),
            pltpu.VMEM((rows, piece), f32),
            pltpu.VMEM((rows, piece), f32),
            pltpu.VMEM((4, rows, piece), f32),
            pltpu.VMEM((2, rows, block), f32),
            pltpu.VMEM((2, 4, group, block), bf16),
            pltpu.VMEM((2, 4, group, block), bf16),
            pltpu.VMEM((2, local, micro, block), bf16),
            dma((3, 4)), dma((3,)), dma((4,)), dma((4,)), dma((4, 2)), dma((4, 2)), dma((3, 4, 2)), dma((3, 4, 2)),
            dma((3, 4, 2)), dma((3, 4, 2)), dma((3, 2)), dma((3, 2)), dma((4, 2)), dma((4, 2)), dma((3, 4)), dma((3, 2)),
            pltpu.SemaphoreType.REGULAR((2,)),
        ],
        compiler_params=pltpu.CompilerParams(collective_id=0, has_side_effects=True, vmem_limit_bytes=56 * 2**20),
    )(
        panels.transpose(1, 0, 2), out_grad.transpose(1, 0, 2),
        gate_weight[0], up_weight[0], down_weight[0],
    )
    grads = weight_updates(x_whole, dy_whole, packed)
    grad = grad.transpose(1, 0, 2)
    return (grad[None], *(g[None] for g in grads))


def fits_kernel(mesh, gate_weight, section_inputs):
    sizes = mesh.shape
    if (sizes["section"], sizes["row"], sizes["col"]) != (2, 4, 4):
        return False
    piece = gate_weight.shape[2] // (sizes["row"] * sizes["col"])
    local = section_inputs.shape[1] * section_inputs.shape[2] // sizes["col"]
    return piece % 128 == 0 and local % 8 == 0 and (local * sizes["col"]) % 32 == 0


def solution(mesh):
    specs = dict(
        mesh=mesh,
        in_specs=(
            P("section", None, "col", "row"),
            P(None, "col", "row"),
            P("section", "row", "col"),
            P("section", "row", "col"),
            P("section", "col", "row"),
        ),
        out_specs=(
            P("section", None, "col", "row"),
            P("section", "row", "col"),
            P("section", "row", "col"),
            P("section", "col", "row"),
        ),
        check_vma=False,
    )

    def run(section_inputs, out_grad, gate_weight, up_weight, down_weight):
        body = fast_shards if fits_kernel(mesh, gate_weight, section_inputs) else shards
        return jax.shard_map(body, **specs)(section_inputs, out_grad, gate_weight, up_weight, down_weight)

    return run
```

time: 88.3 us -> 80.5 us (0.912)
  Pallas kernels: 86 us -> 78.1 us
    pallas_call x1, Pallas kernels: 70.3 us -> 62.5 us  [fast_shards(): pl.pallas_call(relay_kernel, out_shape=(jax.ShapeDtypeStruct(held, bf16),...]
where the time goes in v1:
time: 80.5 us; the launch traced here: 80.2 us
  Pallas kernels  78.1 us (97%)
  local copies, waits for them, and re-layouts  1.45 us (2%)
    pallas_call x1, Pallas kernels, fast_shards(): pl.pallas_call(relay_kernel, out_shape=(jax.ShapeDtypeStruct(held, bf16),...  62.5 us
    pallas_call x1, Pallas kernels, weight_updates(): pl.pallas_call(update_kernel, grid=(hidden_width // tile,), out_shape=(ja...  15.6 us

profile of v1, /device:TPU:0, one launch (start us, length us, event | category | flops | bytes accessed | tf_op | source)
XLA Modules:
  0.0 80.2 jit_solution(6521611125589385849)
XLA Ops:
  0.6 62.5 %shard_map.84 = (bf16[12,2,1024]{2,1,0:T(2,128)(2,1)}, bf16[96,1024]{1,0:T(8,128)(2,1)}, bf16[96,1024]{1,0:T(8,128)(2,1)}, bf16[3,96,3584]{2,1,0:T(8,128)(2,1)}) custom-call(bf16[12,2,1024]{2,1,0:T(2,128)(2,1)} %bitcast.17, bf16[12,2,1024]{2,1,0:T(2,128)(2,1)} %bitcast.18, bf16[1024,3584]{1,0:T(8,128)(2,1)} %bitcast.13, bf16[1024,3584]{1,0:T(8,128)(2,1)} %bitcast.14, ...), custom_call_target="tpu_custom_call" | custom-call | tf_op jit(solution)/shard_map/pallas_call | solution.py:608
  63.1 15.6 %shard_map.85 = (f32[1024,3584]{1,0:T(8,128)}, f32[1024,3584]{1,0:T(8,128)}, f32[3584,1024]{1,0:T(8,128)}) custom-call(bf16[96,1024]{1,0:T(8,128)(2,1)} %get-tuple-element.12.x_ref, bf16[96,1024]{1,0:T(8,128)(2,1)} %get-tuple-element.13.dy_ref, bf16[3,96,3584]{2,1,0:T(8,128)(2,1)} %get-tuple-element.14.packed_ref), custom_call_target="tpu_custom_call" | custom-call | tf_op jit(solution)/shard_map/pallas_call | solution.py:582
  78.8 1.5 %copy.10 = bf16[1,2,12,1024]{3,1,2,0:T(2,128)(2,1)} copy(bf16[1,2,12,1024]{3,1,2,0:T(2,128)(2,1)} %bitcast.16) | data formatting | bytes 98304

commit v2 on v1

v2 whole, which is shorter than its diff:
```python
import jax
import jax.numpy as jnp
from jax import lax
from jax.experimental import pallas as pl
from jax.experimental.pallas import tpu as pltpu
from jax.sharding import PartitionSpec as P

CONTRACT_ROWS = (((0,), (0,)), ((), ()))
CONTRACT_COLS = (((1,), (1,)), ((), ()))


def passed_along(block, axis, distance):
    devices = range(lax.axis_size(axis))
    route = [(i - distance, i) for i in devices if i - distance in devices]
    return lax.ppermute(block, axis, route)


def spread_panel(panel):
    return lax.all_gather(panel, "col", axis=0, tiled=True)


def row_partials(make_terms, keep_rows):
    return lax.psum_scatter(
        make_terms(jnp.int32(0), keep_rows * lax.axis_size("row")).astype(jnp.bfloat16),
        "row",
        scatter_dimension=0,
        tiled=True,
    ).astype(jnp.float32)


def layer_backward(x_local, dy_local, w_both, w_down):
    hidden_width = w_down.shape[0]
    x_whole = spread_panel(x_local)
    dy_whole = spread_panel(dy_local)
    keep_rows = x_whole.shape[0] // lax.axis_size("row")

    def forward_terms(first_row, row_count):
        return jnp.dot(x_whole, w_both, preferred_element_type=jnp.float32)

    def backward_terms(first_row, row_count):
        return lax.dot_general(dy_whole, w_down, CONTRACT_COLS, preferred_element_type=jnp.float32)

    both_sums = row_partials(forward_terms, keep_rows)
    hidden_grad = row_partials(backward_terms, keep_rows)
    gate_sum = both_sums[:, :hidden_width]
    up_sum = both_sums[:, hidden_width:]
    sigmoid_gate = jax.nn.sigmoid(gate_sum)
    activated = gate_sum * sigmoid_gate
    slope = sigmoid_gate * (1.0 + gate_sum * (1.0 - sigmoid_gate))
    hidden = (activated * up_sum).astype(jnp.bfloat16)
    gate_grad = (hidden_grad * up_sum * slope).astype(jnp.bfloat16)
    up_grad = (hidden_grad * activated).astype(jnp.bfloat16)
    packed = jnp.concatenate([hidden, gate_grad, up_grad], axis=1)
    gathered = lax.all_gather(packed, "row", axis=0, tiled=True)
    hidden_whole = gathered[:, :hidden_width]
    both_grads = gathered[:, hidden_width:]
    branch_sum = lax.psum_scatter(
        lax.dot_general(
            both_grads, w_both, CONTRACT_COLS, preferred_element_type=jnp.float32
        ).astype(jnp.bfloat16),
        "col",
        scatter_dimension=0,
        tiled=True,
    ).astype(jnp.float32)
    input_grad = (dy_local.astype(jnp.float32) + branch_sum).astype(jnp.bfloat16)
    down_update = lax.dot_general(
        hidden_whole, dy_whole, CONTRACT_ROWS, preferred_element_type=jnp.float32
    )
    both_update = lax.dot_general(
        x_whole, both_grads, CONTRACT_ROWS, preferred_element_type=jnp.float32
    )
    return (input_grad, both_update, down_update)


def shards(section_inputs, out_grad, gate_weight, up_weight, down_weight):
    section_id = lax.axis_index("section")
    last_section = lax.axis_size("section") - 1
    is_last = section_id == last_section
    panels = section_inputs[0]
    w_both = jnp.concatenate([gate_weight[0], up_weight[0]], axis=1)
    w_down = down_weight[0]
    hidden_width = w_down.shape[0]
    micro_count = panels.shape[0]
    both_total = jnp.zeros(w_both.shape, jnp.float32)
    down_total = jnp.zeros(w_down.shape, jnp.float32)
    merged_shape = (micro_count * panels.shape[1], panels.shape[2])
    x_local = panels.reshape(merged_shape)
    top_grads = out_grad.reshape(merged_shape)
    received = jnp.zeros(merged_shape, jnp.bfloat16)
    merged_results = received
    for step_index in range(last_section + 1):
        is_active = section_id == last_section - step_index
        dy_local = jnp.where(is_last, top_grads, received)
        input_grad, both_update, down_update = layer_backward(x_local, dy_local, w_both, w_down)
        merged_results = jnp.where(is_active, input_grad, merged_results)
        both_total = both_total + jnp.where(is_active, both_update, 0.0)
        down_total = down_total + jnp.where(is_active, down_update, 0.0)
        if step_index < last_section:
            received = passed_along(input_grad, "section", -1)
    results = merged_results.reshape(panels.shape)
    return (
        results[None],
        both_total[:, :hidden_width][None],
        both_total[:, hidden_width:][None],
        down_total[None],
    )


ORDER = pl.DeviceIdType.MESH


def remote(src, dst, send_sem, recv_sem, target):
    return pltpu.make_async_remote_copy(
        src_ref=src, dst_ref=dst, send_sem=send_sem, recv_sem=recv_sem, device_id=target, device_id_type=ORDER
    )


def relay_kernel(
    x_ref, top_ref, gate_ref, up_ref, down_ref,
    x_out, dy_out, packed_out, own_out, far_out_1, far_out_2, far_out_3,
    w_gate, w_up, w_down, turned, x_slots, dy_slots, x_whole, dy_whole, stage, part_send, part_recv, spread, gate_sum, up_sum, factors, middle,
    branch, branch_send, branch_recv, result,
    w_sem, in_sem, send_sem, x_recv_sem, dy_recv_sem, via_sem, pair_sem, last_part_sem,
    first_sem, second_sem, onward_sem, cross_sem, branch_recv_sem, out_sem, go_sem,
):
    section = lax.axis_index("section")
    row = lax.axis_index("row")
    col = lax.axis_index("col")
    rows, width = part_send.shape[2], part_send.shape[3]
    local, micro = x_slots.shape[1:3]
    span = rows // 2
    group = local * micro
    block = x_slots.shape[3] // 2
    is_top = section == 1
    is_bottom = section == 0

    def row_peer(d):
        hi, lo = row // 2, row % 2
        return ((hi + d // 2) % 2) * 2 + (lo + d % 2) % 2

    def ahead(d):
        return (col + d) % 4

    def behind(d):
        return (col + 4 - d) % 4

    def half(h):
        return pl.ds(h * span, span)

    def block_of(c):
        return pl.ds(pl.multiple_of(c * block, block), block)

    def piece_of(d):
        return pl.ds(pl.multiple_of(row_peer(d) * width, width), width)

    weights = ((gate_ref, w_gate), (up_ref, w_up), (down_ref, w_down))

    def weight_load(a):
        source, target = weights[a]
        size = target.shape[0] // 4
        for q in range(4):
            where = pl.ds(q * size, size)
            pltpu.make_async_copy(source.at[where, :], target.at[where, :], w_sem.at[a]).start()

    def weight_wait(a):
        source, target = weights[a]
        pltpu.make_async_copy(source, target, w_sem.at[a]).wait()

    def received(ref, sem):
        remote(ref, ref, send_sem.at[0], sem, (section, row, ahead(1))).wait_recv()

    def sent(ref, kind):
        remote(ref, ref, send_sem.at[kind], send_sem.at[kind], (section, row, ahead(1))).wait_send()

    def x_copy(d):
        return remote(x_slots.at[0], x_slots.at[d], send_sem.at[0], x_recv_sem.at[0], (section, row, ahead(d)))

    def dy_copy(d, c):
        return remote(
            dy_slots.at[c, 0], dy_slots.at[c, d], send_sem.at[1], dy_recv_sem.at[c], (section, row, ahead(d))
        )

    def pass_copy(d, c):
        return remote(result.at[c], dy_slots.at[c, d], send_sem.at[6], dy_recv_sem.at[c], (0, row, ahead(d)))

    def part_copy(a, d, h, via, sem):
        place = (a, d, half(h), slice(None))
        return remote(
            part_send.at[place], part_recv.at[place], send_sem.at[2], sem, (section, row_peer(via), col)
        )

    def via_copy(a, h):
        return part_copy(a, 3, h, 1 + a, via_sem.at[a, h])

    def pair_copy(a, d, h):
        return part_copy(a, d, h, d, pair_sem.at[h])

    def last_part_copy(d, h):
        return part_copy(2, d, h, d, last_part_sem.at[h])

    def relay_sum(a, h):
        middle = 2 - a
        via_copy(a, h).wait_recv()
        total = part_send[a, middle, half(h), :].astype(jnp.float32) + part_recv[a, 3, half(h), :].astype(jnp.float32)
        part_send[a, middle, half(h), :] = total.astype(jnp.bfloat16)
        pair_copy(a, middle, h).start()

    def spread_copy(a, d, h, sem):
        return remote(
            spread.at[a, 0, half(h), :], spread.at[a, d, half(h), :],
            send_sem.at[3], sem, (section, row_peer(d), col),
        )

    def first_copy(a, h):
        d = (1 + h, 1, 2)[a]
        return spread_copy(a, d, h, first_sem.at[a, h])

    def second_copy(a, h):
        d = (2 - h, 2, 1)[a]
        return spread_copy(a, d, h, second_sem.at[a, h if a == 0 else 0])

    def onward_copy(a, h):
        d = (1 + h, 1, 2)[a]
        return remote(
            spread.at[a, d, half(h), :], spread.at[a, 3, half(h), :],
            send_sem.at[4], onward_sem.at[min(a, 1)], (section, row_peer(3 - d), col),
        )

    def spread_grads(h):
        for a in (1, 2):
            first_copy(a, h).start()
        for a in (2, 1):
            second_copy(a, h).start()

    def relay_grads(h):
        for a in (1, 2):
            first_copy(a, h).wait_recv()
            onward_copy(a, h).start()

    def spread_hidden():
        for h in range(2):
            first_copy(0, h).start()
        for h in (1, 0):
            second_copy(0, h).start()

    def relay_hidden():
        for h in range(2):
            first_copy(0, h).wait_recv()
            onward_copy(0, h).start()

    def cross_copy(step, i, h):
        source, target = ((part_send.at[2], part_recv.at[2]), (middle.at[0], middle.at[1]))[step]
        return remote(
            source.at[i, half(h), :], target.at[i, half(h), :],
            send_sem.at[7 + step], cross_sem.at[step, i], (section, row_peer(1 + (step + h) % 2), col),
        )

    def branch_copy(d, c):
        return remote(
            branch_send.at[c, d], branch_recv.at[c, d], send_sem.at[5], branch_recv_sem.at[c], (section, row, behind(d))
        )

    far_outs = (own_out, far_out_1, far_out_2, far_out_3)

    def far_copy(d, c):
        return pltpu.make_async_copy(branch_send.at[c, d], far_outs[d].at[:, block_of(c)], out_sem.at[3])

    def store_copy(a, d):
        return pltpu.make_async_copy(spread.at[a, d], packed_out.at[a, :, piece_of(d)], out_sem.at[0])

    x_store = pltpu.make_async_copy(x_whole, x_out, out_sem.at[1])

    def dy_store(c):
        return pltpu.make_async_copy(dy_whole.at[:, block_of(c)], dy_out.at[:, block_of(c)], out_sem.at[2])

    def merge(slots):
        for d in range(4):
            for t in range(local):
                first = d * group + t * micro
                stage[first:first + micro, :slots.shape[3]] = slots[d, t].astype(jnp.float32)

    x_load = pltpu.make_async_copy(x_ref, x_slots.at[0], in_sem.at[0])

    def top_load(c):
        return pltpu.make_async_copy(top_ref.at[:, :, block_of(c)], dy_slots.at[c, 0], in_sem.at[1 + c])

    x_load.start()

    @pl.when(is_top)
    def _():
        for c in range(2):
            top_load(c).start()

    barrier = pltpu.get_barrier_semaphore()
    greeted = [(section, row, ahead(d)) for d in (1, 2, 3)]
    greeted += [(section, row_peer(d), col) for d in (1, 2, 3)]
    greeted += [(1 - section, row, ahead(d)) for d in range(4)]
    for device in greeted:
        pl.semaphore_signal(barrier, inc=1, device_id=device, device_id_type=ORDER)
    x_load.wait()

    @pl.when(is_top)
    def _():
        for c in range(2):
            top_load(c).wait()

    for a in range(3):
        weight_load(a)

    pl.semaphore_wait(barrier, len(greeted))

    def partner_go(which):
        pl.semaphore_signal(
            go_sem.at[which], inc=1, device_id=(1 - section, row, col), device_id_type=ORDER
        )

    @pl.when(is_bottom)
    def _():
        pl.semaphore_wait(go_sem.at[0], 1)

    for d in (2, 1, 3):
        x_copy(d).start()

    @pl.when(is_top)
    def _():
        for c in range(2):
            for d in (2, 1, 3):
                dy_copy(d, c).start()

    received(x_slots.at[pl.ds(1, 3)], x_recv_sem.at[0])
    merge(x_slots)

    @pl.when(is_top)
    def _():
        partner_go(0)

    x_whole[...] = stage[...].astype(jnp.bfloat16)
    x_store.start()
    for a in range(2):
        weight_wait(a)

    def forward_step(i, carry):
        d = 3 - i
        for a, weight in enumerate((w_gate, w_up)):
            part_send[a, d] = jnp.dot(
                x_whole[...], weight[:, piece_of(d)], preferred_element_type=jnp.float32
            ).astype(jnp.bfloat16)

            @pl.when(jnp.logical_and(is_top, d == 3))
            def _():
                for h in range(2):
                    via_copy(a, h).start()

            @pl.when(jnp.logical_and(is_top, d == 1 + a))
            def _():
                for h in range(2):
                    pair_copy(a, 1 + a, h).start()
        return carry

    lax.fori_loop(0, 4, forward_step, 0)

    def summed(a, where):
        total = part_send[a, 0, where, :].astype(jnp.float32)
        for d in range(1, 4 if a == 2 else 3):
            total = total + part_recv[a, d, where, :].astype(jnp.float32)
        return total

    def rows_of(i):
        return pl.ds(pl.multiple_of(i * 16, 16), 16)

    def sum_step(i, carry):
        where = rows_of(i)
        spread[1, 0, where, :] = summed(0, where).astype(jnp.bfloat16)
        spread[2, 0, where, :] = summed(1, where).astype(jnp.bfloat16)
        return carry

    def hidden_step(i, carry):
        where = rows_of(i)
        gate, up = summed(0, where), summed(1, where)
        gate_sum[where, :] = gate
        up_sum[where, :] = up
        spread[0, 0, where, :] = (gate * jax.nn.sigmoid(gate) * up).astype(jnp.bfloat16)
        return carry

    def factor_rows(first, count):
        def step(k, carry):
            d = first + k // (2 * steps)
            where = rows_of(k % (2 * steps))
            gate = spread[1, d, where, :].astype(jnp.float32)
            up = spread[2, d, where, :].astype(jnp.float32)
            sigmoid_gate = jax.nn.sigmoid(gate)
            activated = gate * sigmoid_gate
            slope = sigmoid_gate * (1.0 + gate * (1.0 - sigmoid_gate))
            spread[0, d, where, :] = (activated * up).astype(jnp.bfloat16)
            factors[0, d, where, :] = up * slope
            factors[1, d, where, :] = activated
            return carry

        lax.fori_loop(0, count * 2 * steps, step, 0)
        for d in range(first, first + count):
            store_copy(0, d).start()

    def grad_step(i, carry):
        where = rows_of(i)
        hidden_grad = summed(2, where)
        gate, up = gate_sum[where, :], up_sum[where, :]
        sigmoid_gate = jax.nn.sigmoid(gate)
        slope = sigmoid_gate * (1.0 + gate * (1.0 - sigmoid_gate))
        spread[1, 0, where, :] = (hidden_grad * up * slope).astype(jnp.bfloat16)
        spread[2, 0, where, :] = (hidden_grad * (gate * sigmoid_gate)).astype(jnp.bfloat16)
        return carry

    steps = span // 16

    def hidden_rows(h):
        received(part_recv.at[pl.ds(0, 2), pl.ds(1, 2), half(h), :], pair_sem.at[h])
        lax.fori_loop(h * steps, (h + 1) * steps, hidden_step, 0)

    def grad_rows(h):
        received(part_recv.at[2, pl.ds(1, 3), half(h), :], last_part_sem.at[h])
        lax.fori_loop(h * steps, (h + 1) * steps, grad_step, 0)
        spread_grads(h)

    @pl.when(is_bottom)
    def _():
        strip = 256 if turned.shape[1] % 256 == 0 else 128

        def turn(k, inner):
            cols = pl.ds(pl.multiple_of(k * strip, strip), strip)
            for a, weight in enumerate((w_gate, w_up)):
                turned[a, cols, :] = weight[:, cols].T
            return inner

        lax.fori_loop(0, turned.shape[1] // strip, turn, 0)
        pl.semaphore_wait(go_sem.at[1], 1)
        for h in range(2):
            for a in range(2):
                via_copy(a, h).start()
        for h in range(2):
            for a in range(2):
                pair_copy(a, 1 + a, h).start()

    for a in range(2):
        relay_sum(a, 0)

    @pl.when(is_bottom)
    def _():
        for a in range(2):
            relay_sum(a, 1)
        for h in range(2):
            received(part_recv.at[pl.ds(0, 2), pl.ds(1, 2), half(h), :], pair_sem.at[h])
            lax.fori_loop(h * steps, (h + 1) * steps, sum_step, 0)
            spread_grads(h)
        relay_grads(0)

    def merge_block(c):
        @pl.when(is_top)
        def _():
            received(dy_slots.at[c, pl.ds(1, 3)], dy_recv_sem.at[c])

        @pl.when(is_bottom)
        def _():
            received(dy_slots.at[c], dy_recv_sem.at[c])

        merge(dy_slots.at[c])
        dy_whole[:, c * block:(c + 1) * block] = stage[:, :block].astype(jnp.bfloat16)
        dy_store(c).start()

    weight_wait(2)

    for c in range(2):
        merge_block(c)

    def grad_terms_step(i, carry):
        d = section * (3 - i) + (1 - section) * i
        owner = section * row_peer(d) + (1 - section) * i
        piece = pl.ds(pl.multiple_of(owner * width, width), width)
        part_send[2, d] = lax.dot_general(
            dy_whole[...], w_down[piece, :], CONTRACT_COLS, preferred_element_type=jnp.float32
        ).astype(jnp.bfloat16)

        @pl.when(is_bottom)
        def _():
            for h in range(2):
                cross_copy(0, i, h).start()

        @pl.when(jnp.logical_and(is_top, d > 0))
        def _():
            last_part_copy(d, 0).start()

        @pl.when(jnp.logical_and(is_top, i == 1))
        def _():
            for a in range(2):
                relay_sum(a, 1)
        return carry

    lax.fori_loop(0, 4, grad_terms_step, 0)

    @pl.when(is_top)
    def _():
        for d in (3, 2, 1):
            last_part_copy(d, 1).start()
        for h in range(2):
            hidden_rows(h)
        for h in range(2):
            grad_rows(h)

    def send_branch(c):
        for d in (2, 3, 1, 0):
            first = d * group
            branch_send[c, d] = branch[first:first + group, c * block:(c + 1) * block].astype(jnp.bfloat16)
            if d:
                @pl.when(is_top)
                def _():
                    branch_copy(d, c).start()
            far_copy(d, c).start()

    def branch_terms(d, cols):
        return lax.dot_general(
            spread[1, d], w_gate[cols, piece_of(d)], CONTRACT_COLS, preferred_element_type=jnp.float32
        ) + lax.dot_general(
            spread[2, d], w_up[cols, piece_of(d)], CONTRACT_COLS, preferred_element_type=jnp.float32
        )

    def branch_step(d, carry):
        @pl.when(d == 1)
        def _():
            for h in range(2):
                relay_grads(h)
            partner_go(1)
            received(spread.at[2, 1], second_sem.at[2, 0])

        @pl.when(d == 2)
        def _():
            received(spread.at[1, 2], second_sem.at[1, 0])

        term = branch_terms(d, slice(None))

        @pl.when(d == 0)
        def _():
            branch[...] = term

        @pl.when(d > 0)
        def _():
            branch[...] += term
        return carry

    def last_branch_step(c, carry):
        @pl.when(c == 1)
        def _():
            send_branch(0)

        branch[:, block_of(c)] += branch_terms(3, block_of(c))
        return carry

    def finish_hidden():
        for h in range(2):
            second_copy(0, h).wait_recv()
        received(spread.at[0, 3], onward_sem.at[0])
        for d in range(4):
            store_copy(0, d).start()

    @pl.when(is_top)
    def _():
        lax.fori_loop(0, 3, branch_step, 0)
        received(spread.at[pl.ds(1, 2), 3], onward_sem.at[1])
        lax.fori_loop(0, 2, last_branch_step, 0)

    def cross_sum(i):
        received(part_recv.at[2, i], cross_sem.at[0, i])
        total = part_send[2, i].astype(jnp.float32) + part_recv[2, i].astype(jnp.float32)
        middle[0, i] = total.astype(jnp.bfloat16)
        for h in range(2):
            cross_copy(1, i, h).start()

    def cross_step(i, carry):
        received(middle.at[1, i], cross_sem.at[1, i])
        d = row_peer(i)

        def grads(k, inner):
            where = rows_of(k)
            hidden_grad = middle[0, i, where, :].astype(jnp.float32) + middle[1, i, where, :].astype(jnp.float32)
            for a in range(2):
                spread[1 + a, d, where, :] = (hidden_grad * factors[a, d, where, :]).astype(jnp.bfloat16)
            return inner

        lax.fori_loop(0, 2 * steps, grads, 0)
        for a in (1, 2):
            store_copy(a, d).start()
        term = jnp.dot(spread[1, d], turned[0, piece_of(d), :], preferred_element_type=jnp.float32)
        term = term + jnp.dot(spread[2, d], turned[1, piece_of(d), :], preferred_element_type=jnp.float32)

        @pl.when(i == 0)
        def _():
            branch[...] = term

        @pl.when(i > 0)
        def _():
            branch[...] += term
        return carry

    @pl.when(is_bottom)
    def _():
        relay_grads(1)
        received(spread.at[2, 1], second_sem.at[2, 0])
        received(spread.at[1, 2], second_sem.at[1, 0])
        factor_rows(0, 3)
        for i in range(4):
            cross_sum(i)
        received(spread.at[pl.ds(1, 2), 3], onward_sem.at[1])
        factor_rows(3, 1)
        sent(spread.at[pl.ds(1, 2), pl.ds(1, 2)], 3)
        sent(spread.at[pl.ds(1, 2), 3], 4)
        lax.fori_loop(0, 4, cross_step, 0)
        send_branch(0)

    send_branch(1)

    @pl.when(is_top)
    def _():
        for c in range(2):
            total = dy_whole[:group, c * block:(c + 1) * block].astype(jnp.float32) + branch[:group, c * block:(c + 1) * block]
            received(branch_recv.at[c, pl.ds(1, 3)], branch_recv_sem.at[c])
            for d in (1, 2, 3):
                total = total + branch_recv[c, d].astype(jnp.float32)
            stage[:group, :block] = total
            for t in range(local):
                result[c, t] = stage[t * micro:(t + 1) * micro, :block].astype(jnp.bfloat16)
            for d in (2, 3, 1, 0):
                pass_copy(d, c).start()
        for a in (1, 2):
            for d in range(4):
                store_copy(a, d).start()
        spread_hidden()
        relay_hidden()
        finish_hidden()
        sent(dy_slots.at[:, pl.ds(1, 3)], 1)
        sent(dy_slots, 6)
        sent(branch_send.at[:, pl.ds(1, 3)], 5)
        sent(part_send.at[:, pl.ds(1, 3)], 2)
        sent(spread.at[:, pl.ds(1, 2)], 3)
        sent(spread.at[:, 3], 4)

    @pl.when(is_bottom)
    def _():
        sent(part_send.at[pl.ds(0, 2), pl.ds(1, 3)], 2)
        sent(part_send.at[2], 7)
        sent(middle.at[0], 8)

    sent(x_slots.at[pl.ds(1, 3)], 0)
    pltpu.make_async_copy(spread, spread, out_sem.at[0]).wait()
    x_store.wait()
    pltpu.make_async_copy(dy_whole, dy_whole, out_sem.at[2]).wait()
    pltpu.make_async_copy(branch_send, branch_send, out_sem.at[3]).wait()


def update_kernel(
    x_ref, dy_ref, packed_ref, gate_out, up_out, down_out,
    x_held, dy_held, packed_held, gate_tiles, up_tiles, down_tiles, in_sem, sem,
):
    loads = [
        pltpu.make_async_copy(x_ref, x_held, in_sem.at[0]),
        pltpu.make_async_copy(packed_ref.at[1], packed_held.at[1], in_sem.at[1]),
        pltpu.make_async_copy(packed_ref.at[2], packed_held.at[2], in_sem.at[2]),
        pltpu.make_async_copy(packed_ref.at[0], packed_held.at[0], in_sem.at[3]),
        pltpu.make_async_copy(dy_ref, dy_held, in_sem.at[4]),
    ]
    for load in loads:
        load.start()

    def tiles_of(left, right, tiles, target, done):
        size = tiles.shape[1]

        def step(j, carry):
            where = pl.ds(pl.multiple_of(j * size, size), size)
            tiles[j] = lax.dot_general(left[:, where], right[...], CONTRACT_ROWS, preferred_element_type=jnp.float32)
            pltpu.make_async_copy(tiles.at[j], target.at[where, :], done).start()
            return carry

        lax.fori_loop(0, tiles.shape[0], step, 0)

    loads[0].wait()
    loads[1].wait()
    tiles_of(x_held, packed_held.at[1], gate_tiles, gate_out, sem.at[0])
    loads[2].wait()
    tiles_of(x_held, packed_held.at[2], up_tiles, up_out, sem.at[1])
    loads[3].wait()
    loads[4].wait()
    tiles_of(packed_held.at[0], dy_held, down_tiles, down_out, sem.at[2])
    for a, tiles in enumerate((gate_tiles, up_tiles, down_tiles)):
        pltpu.make_async_copy(tiles, tiles, sem.at[a]).wait()


def weight_updates(x_whole, dy_whole, packed):
    rows, width = x_whole.shape
    hidden_width = packed.shape[2]
    tall, wide = (next(t for t in (256, 128) if n % t == 0) for n in (hidden_width, width))
    f32 = jnp.float32
    hbm = pl.BlockSpec(memory_space=pltpu.HBM)
    return pl.pallas_call(
        update_kernel,
        out_shape=(
            jax.ShapeDtypeStruct((width, hidden_width), f32),
            jax.ShapeDtypeStruct((width, hidden_width), f32),
            jax.ShapeDtypeStruct((hidden_width, width), f32),
        ),
        in_specs=[hbm, hbm, hbm],
        out_specs=(hbm, hbm, hbm),
        scratch_shapes=[
            pltpu.VMEM((rows, width), jnp.bfloat16),
            pltpu.VMEM((rows, width), jnp.bfloat16),
            pltpu.VMEM((3, rows, hidden_width), jnp.bfloat16),
            pltpu.VMEM((width // wide, wide, hidden_width), f32),
            pltpu.VMEM((width // wide, wide, hidden_width), f32),
            pltpu.VMEM((hidden_width // tall, tall, width), f32),
            pltpu.SemaphoreType.DMA((5,)),
            pltpu.SemaphoreType.DMA((3,)),
        ],
        compiler_params=pltpu.CompilerParams(vmem_limit_bytes=67043328),
        cost_estimate=pl.CostEstimate(
            flops=6 * rows * width * hidden_width,
            bytes_accessed=12 * width * hidden_width + 2 * rows * (2 * width + 3 * hidden_width),
            transcendentals=0,
        ),
    )(x_whole, dy_whole, packed)


def fast_shards(section_inputs, out_grad, gate_weight, up_weight, down_weight):
    panels = section_inputs[0]
    micro, local, width = panels.shape
    group = micro * local
    held = (local, micro, width)
    rows = group * lax.axis_size("col")
    hidden_width = gate_weight.shape[2]
    piece = hidden_width // lax.axis_size("row")
    hbm = pl.BlockSpec(memory_space=pltpu.HBM)
    bf16, f32 = jnp.bfloat16, jnp.float32
    dma = pltpu.SemaphoreType.DMA
    block = width // 2
    far = jax.ShapeDtypeStruct((group, width), bf16)
    x_whole, dy_whole, packed, own, *far_terms = pl.pallas_call(
        relay_kernel,
        out_shape=(
            jax.ShapeDtypeStruct((rows, width), bf16),
            jax.ShapeDtypeStruct((rows, width), bf16),
            jax.ShapeDtypeStruct((3, rows, hidden_width), bf16),
            far, far, far, far,
        ),
        in_specs=[hbm] * 5,
        out_specs=(hbm,) * 7,
        scratch_shapes=[
            pltpu.VMEM((width, hidden_width), bf16),
            pltpu.VMEM((width, hidden_width), bf16),
            pltpu.VMEM((hidden_width, width), bf16),
            pltpu.VMEM((2, hidden_width, width), bf16),
            pltpu.VMEM((4, *held), bf16),
            pltpu.VMEM((2, 4, local, micro, block), bf16),
            pltpu.VMEM((rows, width), bf16),
            pltpu.VMEM((rows, width), bf16),
            pltpu.VMEM((rows, width), f32),
            pltpu.VMEM((3, 4, rows, piece), bf16),
            pltpu.VMEM((3, 4, rows, piece), bf16),
            pltpu.VMEM((3, 4, rows, piece), bf16),
            pltpu.VMEM((rows, piece), f32),
            pltpu.VMEM((rows, piece), f32),
            pltpu.VMEM((2, 4, rows, piece), f32),
            pltpu.VMEM((2, 4, rows, piece), bf16),
            pltpu.VMEM((rows, width), f32),
            pltpu.VMEM((2, 4, group, block), bf16),
            pltpu.VMEM((2, 4, group, block), bf16),
            pltpu.VMEM((2, local, micro, block), bf16),
            dma((3,)), dma((3,)), dma((9,)), dma((1,)), dma((2,)), dma((2, 2)), dma((2,)), dma((2,)),
            dma((3, 2)), dma((3, 2)), dma((2,)), dma((2, 4)), dma((2,)), dma((4,)), pltpu.SemaphoreType.REGULAR((2,)),
        ],
        compiler_params=pltpu.CompilerParams(collective_id=0, has_side_effects=True, vmem_limit_bytes=60 * 2**20),
    )(
        panels.transpose(1, 0, 2), out_grad.transpose(1, 0, 2),
        gate_weight[0], up_weight[0], down_weight[0],
    )
    cols = lax.axis_size("col")
    arrived = [
        lax.ppermute(term, "col", [(i, (i + cols - d) % cols) for i in range(cols)])
        for d, term in zip((1, 2, 3), far_terms, strict=True)
    ]
    grads = weight_updates(x_whole, dy_whole, packed)
    grad = dy_whole[:group].astype(f32) + own.astype(f32)
    for term in arrived:
        grad = grad + term.astype(f32)
    grad = grad.astype(bf16).reshape(held).transpose(1, 0, 2)
    return (grad[None], *(g[None] for g in grads))


def fits_kernel(mesh, gate_weight, section_inputs):
    sizes = mesh.shape
    if (sizes["section"], sizes["row"], sizes["col"]) != (2, 4, 4):
        return False
    piece = gate_weight.shape[2] // (sizes["row"] * sizes["col"])
    local = section_inputs.shape[1] * section_inputs.shape[2] // sizes["col"]
    return piece % 128 == 0 and section_inputs.shape[3] % (256 * sizes["row"]) == 0 and local % 8 == 0 and (local * sizes["col"]) % 32 == 0


def solution(mesh):
    specs = dict(
        mesh=mesh,
        in_specs=(
            P("section", None, "col", "row"),
            P(None, "col", "row"),
            P("section", "row", "col"),
            P("section", "row", "col"),
            P("section", "col", "row"),
        ),
        out_specs=(
            P("section", None, "col", "row"),
            P("section", "row", "col"),
            P("section", "row", "col"),
            P("section", "col", "row"),
        ),
        check_vma=False,
    )

    def run(section_inputs, out_grad, gate_weight, up_weight, down_weight):
        body = fast_shards if fits_kernel(mesh, gate_weight, section_inputs) else shards
        return jax.shard_map(body, **specs)(section_inputs, out_grad, gate_weight, up_weight, down_weight)

    return run
```

time: 80.5 us -> 75 us (0.932)
  Pallas kernels: 78.1 us -> 69.2 us
  starting transfers between devices: 0 us -> 3.28 us
  other arithmetic: 0 us -> 0.93 us
  local copies, waits for them, and re-layouts: 1.45 us -> 0.64 us
    pallas_call x2, Pallas kernels: 78.1 us -> 69.2 us  [the longest x1 53.1 us: fast_shards(): pl.pallas_call(relay_kernel, out_shape=(jax.ShapeDtypeStruct((rows, width...]
    ppermute x0 -> x3, starting transfers between devices: none -> 3.28 us  [fast_shards(): lax.ppermute(term, 'col', [(i, (i + cols - d) % cols) for i in range(cols)])]
    unnamed x1 -> x0, local copies, waits for them, and re-layouts: 1.45 us -> none
    convert_element_type x0 -> x1, other arithmetic: none -> 0.93 us  [fast_shards(): grad = grad.astype(bf16).reshape(held).transpose(1, 0, 2)]
  transfers between devices with their start and end apart: 0 -> 3, of which waited for: 0 -> 0; matrix products, arithmetic and copies ran while one was open for 0% -> 0% of each run, Pallas kernels for 0% -> 21%
where the time goes in v2:
time: 75 us; the launch traced here: 74.7 us
  Pallas kernels  69.2 us (92%)
  starting transfers between devices  3.28 us (4%)
  other arithmetic  0.93 us (1%)
    pallas_call x1, Pallas kernels, fast_shards(): pl.pallas_call(relay_kernel, out_shape=(jax.ShapeDtypeStruct((rows, width...  53.1 us
    pallas_call x1, Pallas kernels, weight_updates(): pl.pallas_call(update_kernel, out_shape=(jax.ShapeDtypeStruct((width, hid...  16 us
    ppermute x3, starting transfers between devices, fast_shards(): lax.ppermute(term, 'col', [(i, (i + cols - d) % cols) for i in range(cols)])  3.28 us
  transfers between devices with their start and end apart: 3, of which 0 were waited for; matrix products, arithmetic and copies ran while one was open for 0% of the time, Pallas kernels for 21%

profile of v2, /device:TPU:0, one launch (start us, length us, event | category | flops | bytes accessed | tf_op | source)
XLA Modules:
  0.0 74.7 jit_solution(16342274359109062783)
XLA Ops:
  0.6 53.1 %shard_map.84 = (bf16[96,1024]{1,0:T(8,128)(2,1)}, bf16[96,1024]{1,0:T(8,128)(2,1)}, bf16[3,96,3584]{2,1,0:T(8,128)(2,1)}, bf16[24,1024]{1,0:T(8,128)(2,1)}, bf1...) custom-call(bf16[12,2,1024]{2,1,0:T(2,128)(2,1)} %bitcast.17, ...), custom_call_target="tpu_custom_call" | custom-call | tf_op jit(solution)/shard_map/pallas_call | solution.py:741
  53.8 2.1 %collective-permute-start = (bf16[24,1024]{1,0:T(8,128)(2,1)}, bf16[24,1024]{1,0:T(8,128)(2,1)}, u32[]{:S(2)}, u32[]{:S(2)}) collective-permute-start(bf16[24,1024]{1,0:T(8,128)(2,1)} %get-tuple-element.16), channel_id=1, source_target_pairs={{0,3},{1,0},{2,1},{3,2},{4,7},{5,4},{6,5},{7,6},{8,11},{9,8},{10,9... | collective-permute-start | bytes 147464 | tf_op jit(solution)/shard_map/ppermute | solution.py:782
  55.9 0.2 collective-permute-start.1
  56.1 0.9 %collective-permute-start.2 = (bf16[24,1024]{1,0:T(8,128)(2,1)}, bf16[24,1024]{1,0:T(8,128)(2,1)}, u32[]{:S(2)}, u32[]{:S(2)}) collective-permute-start(bf16[24,1024]{1,0:T(8,128)(2,1)} %get-tuple-element.18), channel_id=1, source_target_pairs={{0,1},{1,2},{2,3},{3,0},{4,5},{5,6},{6,7},{7,4},{8,9},{9,10},{10,1... | collective-permute-start | bytes 147464 | tf_op jit(solution)/shard_map/ppermute | solution.py:782
  57.1 16.0 %shard_map.85 = (f32[1024,3584]{1,0:T(8,128)}, f32[1024,3584]{1,0:T(8,128)}, f32[3584,1024]{1,0:T(8,128)}) custom-call(bf16[96,1024]{1,0:T(8,128)(2,1)} %get-tuple-element.19.x_ref, bf16[96,1024]{1,0:T(8,128)(2,1)} %get-tuple-element.14.dy_ref, bf16[3,96,3584]{2,1,0:T(8,128)(2,1)} %get-tuple-element.20.packed_ref), custom_call_target="tpu_custom_call" | custom-call | flops 2113929216 | bytes 46497792 | tf_op jit(solution)/shard_map/pallas_call | solution.py:700
  73.1 0.0 collective-permute-done
  73.1 0.0 collective-permute-done.1
  73.1 0.0 collective-permute-done.2
  73.1 0.9 %add_convert_fusion = bf16[24,1024]{1,0:T(8,128)(2,1)S(1)} fusion(bf16[24,1024]{1,0:T(8,128)(2,1)} %collective-permute-done.2, bf16[24,1024]{1,0:T(8,128)(2,1)} %collective-permute-done.1, bf16[24,1024]{1,0:T(8,128)(2,1)} %collective-permute-done, bf16[24,1024]{1,0:T(8,128)(2,1)} %get-tuple-element.15, bf16[96,1024]{1,0:T(8,128)(2,1)} %get-tuple-element.14.dy_ref), kind=kLoop, calls=%fused_computation | loop fusion | flops 245760 | bytes 294912 | tf_op jit(solution)/shard_map/convert_element_type | solution.py:789
  74.1 0.6 reshape.11
Async XLA Ops:
  53.8 19.3 %collective-permute-start = (bf16[24,1024]{1,0:T(8,128)(2,1)}, bf16[24,1024]{1,0:T(8,128)(2,1)}, u32[]{:S(2)}, u32[]{:S(2)}) collective-permute-start(bf16[24,1024]{1,0:T(8,128)(2,1)} %get-tuple-element.16), channel_id=1, source_target_pairs={{0,3},{1,0},{2,1},{3,2},{4,7},{5,4},{6,5},{7,6},{8,11},{9,8},{10,9... | collective-permute-start | bytes 147464 | tf_op jit(solution)/shard_map/ppermute | solution.py:782
  55.9 17.2 %collective-permute-start.1 = (bf16[24,1024]{1,0:T(8,128)(2,1)}, bf16[24,1024]{1,0:T(8,128)(2,1)}, u32[]{:S(2)}, u32[]{:S(2)}) collective-permute-start(bf16[24,1024]{1,0:T(8,128)(2,1)} %get-tuple-element.17), channel_id=1, source_target_pairs={{0,2},{1,3},{2,0},{3,1},{4,6},{5,7},{6,4},{7,5},{8,10},{9,11},{10,... | collective-permute-start | bytes 147464 | tf_op jit(solution)/shard_map/ppermute | solution.py:782
  56.1 17.0 %collective-permute-start.2 = (bf16[24,1024]{1,0:T(8,128)(2,1)}, bf16[24,1024]{1,0:T(8,128)(2,1)}, u32[]{:S(2)}, u32[]{:S(2)}) collective-permute-start(bf16[24,1024]{1,0:T(8,128)(2,1)} %get-tuple-element.18), channel_id=1, source_target_pairs={{0,1},{1,2},{2,3},{3,0},{4,5},{5,6},{6,7},{7,4},{8,9},{9,10},{10,1... | collective-permute-start | bytes 147464 | tf_op jit(solution)/shard_map/ppermute | solution.py:782

commit v3 on v2

--- a/solution.py
+++ b/solution.py
@@ -117,11 +117,11 @@
 
 def relay_kernel(
     x_ref, top_ref, gate_ref, up_ref, down_ref,
-    x_out, dy_out, packed_out, own_out, far_out_1, far_out_2, far_out_3,
-    w_gate, w_up, w_down, turned, x_slots, dy_slots, x_whole, dy_whole, stage, part_send, part_recv, spread, gate_sum, up_sum, factors, middle,
-    branch, branch_send, branch_recv, result,
+    x_whole, dy_whole, spread, result,
+    w_gate, w_up, w_down, turned, x_slots, dy_slots, stage, part_send, part_recv, gate_sum, up_sum, factors, middle,
+    branch, branch_send, branch_recv,
     w_sem, in_sem, send_sem, x_recv_sem, dy_recv_sem, via_sem, pair_sem, last_part_sem,
-    first_sem, second_sem, onward_sem, cross_sem, branch_recv_sem, out_sem, go_sem,
+    first_sem, second_sem, onward_sem, cross_sem, branch_recv_sem, go_sem,
 ):
     section = lax.axis_index("section")
     row = lax.axis_index("row")
@@ -131,6 +131,7 @@
     span = rows // 2
     group = local * micro
     block = x_slots.shape[3] // 2
+    own = row
     is_top = section == 1
     is_bottom = section == 0
 
@@ -181,7 +182,7 @@
         )
 
     def pass_copy(d, c):
-        return remote(result.at[c], dy_slots.at[c, d], send_sem.at[6], dy_recv_sem.at[c], (0, row, ahead(d)))
+        return remote(result.at[:, :, block_of(c)], dy_slots.at[c, d], send_sem.at[6], dy_recv_sem.at[c], (0, row, ahead(d)))
 
     def part_copy(a, d, h, via, sem):
         place = (a, d, half(h), slice(None))
@@ -205,24 +206,22 @@
         part_send[a, middle, half(h), :] = total.astype(jnp.bfloat16)
         pair_copy(a, middle, h).start()
 
-    def spread_copy(a, d, h, sem):
-        return remote(
-            spread.at[a, 0, half(h), :], spread.at[a, d, half(h), :],
-            send_sem.at[3], sem, (section, row_peer(d), col),
-        )
-
-    def first_copy(a, h):
+    def spread_copy(a, piece, d, h, sem):
+        place = (a, piece, half(h), slice(None))
+        return remote(spread.at[place], spread.at[place], send_sem.at[3], sem, (section, row_peer(d), col))
+
+    def first_copy(a, h, piece=None):
         d = (1 + h, 1, 2)[a]
-        return spread_copy(a, d, h, first_sem.at[a, h])
-
-    def second_copy(a, h):
+        return spread_copy(a, own if piece is None else row_peer(d), d, h, first_sem.at[a, h])
+
+    def second_copy(a, h, piece=None):
         d = (2 - h, 2, 1)[a]
-        return spread_copy(a, d, h, second_sem.at[a, h if a == 0 else 0])
+        return spread_copy(a, own if piece is None else row_peer(d), d, h, second_sem.at[a, h if a == 0 else 0])
 
     def onward_copy(a, h):
         d = (1 + h, 1, 2)[a]
         return remote(
-            spread.at[a, d, half(h), :], spread.at[a, 3, half(h), :],
+            spread.at[a, row_peer(d), half(h), :], spread.at[a, row_peer(d), half(h), :],
             send_sem.at[4], onward_sem.at[min(a, 1)], (section, row_peer(3 - d), col),
         )
 
@@ -234,7 +233,7 @@
 
     def relay_grads(h):
         for a in (1, 2):
-            first_copy(a, h).wait_recv()
+            first_copy(a, h, 1).wait_recv()
             onward_copy(a, h).start()
 
     def spread_hidden():
@@ -245,7 +244,7 @@
 
     def relay_hidden():
         for h in range(2):
-            first_copy(0, h).wait_recv()
+            first_copy(0, h, 1).wait_recv()
             onward_copy(0, h).start()
 
     def cross_copy(step, i, h):
@@ -259,19 +258,6 @@
         return remote(
             branch_send.at[c, d], branch_recv.at[c, d], send_sem.at[5], branch_recv_sem.at[c], (section, row, behind(d))
         )
-
-    far_outs = (own_out, far_out_1, far_out_2, far_out_3)
-
-    def far_copy(d, c):
-        return pltpu.make_async_copy(branch_send.at[c, d], far_outs[d].at[:, block_of(c)], out_sem.at[3])
-
-    def store_copy(a, d):
-        return pltpu.make_async_copy(spread.at[a, d], packed_out.at[a, :, piece_of(d)], out_sem.at[0])
-
-    x_store = pltpu.make_async_copy(x_whole, x_out, out_sem.at[1])
-
-    def dy_store(c):
-        return pltpu.make_async_copy(dy_whole.at[:, block_of(c)], dy_out.at[:, block_of(c)], out_sem.at[2])
 
     def merge(slots):
         for d in range(4):
@@ -335,7 +321,6 @@
         partner_go(0)
 
     x_whole[...] = stage[...].astype(jnp.bfloat16)
-    x_store.start()
     for a in range(2):
         weight_wait(a)
 
@@ -370,8 +355,8 @@
 
     def sum_step(i, carry):
         where = rows_of(i)
-        spread[1, 0, where, :] = summed(0, where).astype(jnp.bfloat16)
-        spread[2, 0, where, :] = summed(1, where).astype(jnp.bfloat16)
+        spread[1, own, where, :] = summed(0, where).astype(jnp.bfloat16)
+        spread[2, own, where, :] = summed(1, where).astype(jnp.bfloat16)
         return carry
 
     def hidden_step(i, carry):
@@ -379,12 +364,12 @@
         gate, up = summed(0, where), summed(1, where)
         gate_sum[where, :] = gate
         up_sum[where, :] = up
-        spread[0, 0, where, :] = (gate * jax.nn.sigmoid(gate) * up).astype(jnp.bfloat16)
+        spread[0, own, where, :] = (gate * jax.nn.sigmoid(gate) * up).astype(jnp.bfloat16)
         return carry
 
     def factor_rows(first, count):
         def step(k, carry):
-            d = first + k // (2 * steps)
+            d = row_peer(first + k // (2 * steps))
             where = rows_of(k % (2 * steps))
             gate = spread[1, d, where, :].astype(jnp.float32)
             up = spread[2, d, where, :].astype(jnp.float32)
@@ -397,8 +382,6 @@
             return carry
 
         lax.fori_loop(0, count * 2 * steps, step, 0)
-        for d in range(first, first + count):
-            store_copy(0, d).start()
 
     def grad_step(i, carry):
         where = rows_of(i)
@@ -406,8 +389,8 @@
         gate, up = gate_sum[where, :], up_sum[where, :]
         sigmoid_gate = jax.nn.sigmoid(gate)
         slope = sigmoid_gate * (1.0 + gate * (1.0 - sigmoid_gate))
-        spread[1, 0, where, :] = (hidden_grad * up * slope).astype(jnp.bfloat16)
-        spread[2, 0, where, :] = (hidden_grad * (gate * sigmoid_gate)).astype(jnp.bfloat16)
+        spread[1, own, where, :] = (hidden_grad * up * slope).astype(jnp.bfloat16)
+        spread[2, own, where, :] = (hidden_grad * (gate * sigmoid_gate)).astype(jnp.bfloat16)
         return carry
 
     steps = span // 16
@@ -464,7 +447,6 @@
 
         merge(dy_slots.at[c])
         dy_whole[:, c * block:(c + 1) * block] = stage[:, :block].astype(jnp.bfloat16)
-        dy_store(c).start()
 
     weight_wait(2)
 
@@ -506,20 +488,16 @@
             grad_rows(h)
 
     def send_branch(c):
-        for d in (2, 3, 1, 0):
+        for d in (2, 3, 1):
             first = d * group
             branch_send[c, d] = branch[first:first + group, c * block:(c + 1) * block].astype(jnp.bfloat16)
-            if d:
-                @pl.when(is_top)
-                def _():
-                    branch_copy(d, c).start()
-            far_copy(d, c).start()
+            branch_copy(d, c).start()
 
     def branch_terms(d, cols):
         return lax.dot_general(
-            spread[1, d], w_gate[cols, piece_of(d)], CONTRACT_COLS, preferred_element_type=jnp.float32
+            spread[1, row_peer(d)], w_gate[cols, piece_of(d)], CONTRACT_COLS, preferred_element_type=jnp.float32
         ) + lax.dot_general(
-            spread[2, d], w_up[cols, piece_of(d)], CONTRACT_COLS, preferred_element_type=jnp.float32
+            spread[2, row_peer(d)], w_up[cols, piece_of(d)], CONTRACT_COLS, preferred_element_type=jnp.float32
         )
 
     def branch_step(d, carry):
@@ -528,11 +506,11 @@
             for h in range(2):
                 relay_grads(h)
             partner_go(1)
-            received(spread.at[2, 1], second_sem.at[2, 0])
+            received(spread.at[2, row_peer(1)], second_sem.at[2, 0])
 
         @pl.when(d == 2)
         def _():
-            received(spread.at[1, 2], second_sem.at[1, 0])
+            received(spread.at[1, row_peer(2)], second_sem.at[1, 0])
 
         term = branch_terms(d, slice(None))
 
@@ -555,15 +533,13 @@
 
     def finish_hidden():
         for h in range(2):
-            second_copy(0, h).wait_recv()
-        received(spread.at[0, 3], onward_sem.at[0])
-        for d in range(4):
-            store_copy(0, d).start()
+            second_copy(0, h, 1).wait_recv()
+        received(spread.at[0, row_peer(3)], onward_sem.at[0])
 
     @pl.when(is_top)
     def _():
         lax.fori_loop(0, 3, branch_step, 0)
-        received(spread.at[pl.ds(1, 2), 3], onward_sem.at[1])
+        received(spread.at[pl.ds(1, 2), row_peer(3)], onward_sem.at[1])
         lax.fori_loop(0, 2, last_branch_step, 0)
 
     def cross_sum(i):
@@ -573,22 +549,26 @@
         for h in range(2):
             cross_copy(1, i, h).start()
 
-    def cross_step(i, carry):
+    def cross_grads(i):
         received(middle.at[1, i], cross_sem.at[1, i])
-        d = row_peer(i)
-
-        def grads(k, inner):
+
+        def grads(k, carry):
             where = rows_of(k)
             hidden_grad = middle[0, i, where, :].astype(jnp.float32) + middle[1, i, where, :].astype(jnp.float32)
             for a in range(2):
-                spread[1 + a, d, where, :] = (hidden_grad * factors[a, d, where, :]).astype(jnp.bfloat16)
-            return inner
+                spread[1 + a, i, where, :] = (hidden_grad * factors[a, i, where, :]).astype(jnp.bfloat16)
+            return carry
 
         lax.fori_loop(0, 2 * steps, grads, 0)
-        for a in (1, 2):
-            store_copy(a, d).start()
-        term = jnp.dot(spread[1, d], turned[0, piece_of(d), :], preferred_element_type=jnp.float32)
-        term = term + jnp.dot(spread[2, d], turned[1, piece_of(d), :], preferred_element_type=jnp.float32)
+
+    def turned_terms(i, cols):
+        piece = pl.ds(i * width if isinstance(i, int) else pl.multiple_of(i * width, width), width)
+        term = jnp.dot(spread[1, i], turned[0, piece, cols], preferred_element_type=jnp.float32)
+        return term + jnp.dot(spread[2, i], turned[1, piece, cols], preferred_element_type=jnp.float32)
+
+    def cross_step(i, carry):
+        cross_grads(i)
+        term = turned_terms(i, slice(None))
 
         @pl.when(i == 0)
         def _():
@@ -599,44 +579,56 @@
             branch[...] += term
         return carry
 
+    def last_cross_step(c, carry):
+        @pl.when(c == 1)
+        def _():
+            send_branch(0)
+
+        branch[:, block_of(c)] += turned_terms(3, block_of(c))
+        return carry
+
     @pl.when(is_bottom)
     def _():
         relay_grads(1)
-        received(spread.at[2, 1], second_sem.at[2, 0])
-        received(spread.at[1, 2], second_sem.at[1, 0])
+        received(spread.at[2, row_peer(1)], second_sem.at[2, 0])
+        received(spread.at[1, row_peer(2)], second_sem.at[1, 0])
         factor_rows(0, 3)
         for i in range(4):
             cross_sum(i)
-        received(spread.at[pl.ds(1, 2), 3], onward_sem.at[1])
+        partner_go(2)
+        received(spread.at[pl.ds(1, 2), row_peer(3)], onward_sem.at[1])
         factor_rows(3, 1)
         sent(spread.at[pl.ds(1, 2), pl.ds(1, 2)], 3)
         sent(spread.at[pl.ds(1, 2), 3], 4)
-        lax.fori_loop(0, 4, cross_step, 0)
-        send_branch(0)
+        lax.fori_loop(0, 3, cross_step, 0)
+        cross_grads(3)
+        lax.fori_loop(0, 2, last_cross_step, 0)
 
     send_branch(1)
 
-    @pl.when(is_top)
-    def _():
-        for c in range(2):
-            total = dy_whole[:group, c * block:(c + 1) * block].astype(jnp.float32) + branch[:group, c * block:(c + 1) * block]
-            received(branch_recv.at[c, pl.ds(1, 3)], branch_recv_sem.at[c])
-            for d in (1, 2, 3):
-                total = total + branch_recv[c, d].astype(jnp.float32)
-            stage[:group, :block] = total
-            for t in range(local):
-                result[c, t] = stage[t * micro:(t + 1) * micro, :block].astype(jnp.bfloat16)
+    for c in range(2):
+        cols = slice(c * block, (c + 1) * block)
+        total = dy_whole[:group, cols].astype(jnp.float32) + branch[:group, cols]
+        received(branch_recv.at[c, pl.ds(1, 3)], branch_recv_sem.at[c])
+        for d in (1, 2, 3):
+            total = total + branch_recv[c, d].astype(jnp.float32)
+        stage[:group, :block] = total
+        for t in range(local):
+            result[t, :, cols] = stage[t * micro:(t + 1) * micro, :block].astype(jnp.bfloat16)
+
+        @pl.when(is_top)
+        def _():
             for d in (2, 3, 1, 0):
                 pass_copy(d, c).start()
-        for a in (1, 2):
-            for d in range(4):
-                store_copy(a, d).start()
+
+    @pl.when(is_top)
+    def _():
+        pl.semaphore_wait(go_sem.at[2], 1)
         spread_hidden()
         relay_hidden()
         finish_hidden()
         sent(dy_slots.at[:, pl.ds(1, 3)], 1)
         sent(dy_slots, 6)
-        sent(branch_send.at[:, pl.ds(1, 3)], 5)
         sent(part_send.at[:, pl.ds(1, 3)], 2)
         sent(spread.at[:, pl.ds(1, 2)], 3)
         sent(spread.at[:, 3], 4)
@@ -647,55 +639,49 @@
         sent(part_send.at[2], 7)
         sent(middle.at[0], 8)
 
+    sent(branch_send.at[:, pl.ds(1, 3)], 5)
     sent(x_slots.at[pl.ds(1, 3)], 0)
-    pltpu.make_async_copy(spread, spread, out_sem.at[0]).wait()
-    x_store.wait()
-    pltpu.make_async_copy(dy_whole, dy_whole, out_sem.at[2]).wait()
-    pltpu.make_async_copy(branch_send, branch_send, out_sem.at[3]).wait()
-
-
-def update_kernel(
-    x_ref, dy_ref, packed_ref, gate_out, up_out, down_out,
-    x_held, dy_held, packed_held, gate_tiles, up_tiles, down_tiles, in_sem, sem,
-):
-    loads = [
-        pltpu.make_async_copy(x_ref, x_held, in_sem.at[0]),
-        pltpu.make_async_copy(packed_ref.at[1], packed_held.at[1], in_sem.at[1]),
-        pltpu.make_async_copy(packed_ref.at[2], packed_held.at[2], in_sem.at[2]),
-        pltpu.make_async_copy(packed_ref.at[0], packed_held.at[0], in_sem.at[3]),
-        pltpu.make_async_copy(dy_ref, dy_held, in_sem.at[4]),
-    ]
-    for load in loads:
-        load.start()
-
-    def tiles_of(left, right, tiles, target, done):
-        size = tiles.shape[1]
-
-        def step(j, carry):
-            where = pl.ds(pl.multiple_of(j * size, size), size)
-            tiles[j] = lax.dot_general(left[:, where], right[...], CONTRACT_ROWS, preferred_element_type=jnp.float32)
-            pltpu.make_async_copy(tiles.at[j], target.at[where, :], done).start()
-            return carry
-
-        lax.fori_loop(0, tiles.shape[0], step, 0)
-
-    loads[0].wait()
-    loads[1].wait()
-    tiles_of(x_held, packed_held.at[1], gate_tiles, gate_out, sem.at[0])
-    loads[2].wait()
-    tiles_of(x_held, packed_held.at[2], up_tiles, up_out, sem.at[1])
-    loads[3].wait()
-    loads[4].wait()
-    tiles_of(packed_held.at[0], dy_held, down_tiles, down_out, sem.at[2])
-    for a, tiles in enumerate((gate_tiles, up_tiles, down_tiles)):
+
+def update_kernel(x_ref, dy_ref, packed_ref, gate_out, up_out, down_out, wide_tiles, down_tiles, sem):
+    pieces, rows, piece = packed_ref.shape[1:]
+    tall = wide_tiles.shape[2]
+
+    def wide_step(k, carry):
+        a = k // wide_tiles.shape[1]
+        j = k % wide_tiles.shape[1]
+        where = pl.ds(pl.multiple_of(j * tall, tall), tall)
+
+        for p in range(pieces):
+            wide_tiles[a, j, :, p * piece:(p + 1) * piece] = lax.dot_general(
+                x_ref[:, where], packed_ref[1 + a, p], CONTRACT_ROWS, preferred_element_type=jnp.float32
+            )
+        for b, target in enumerate((gate_out, up_out)):
+            @pl.when(a == b)
+            def _():
+                pltpu.make_async_copy(wide_tiles.at[b, j], target.at[where, :], sem.at[b]).start()
+        return carry
+
+    lax.fori_loop(0, 2 * wide_tiles.shape[1], wide_step, 0)
+    def down_step(p, carry):
+        where = pl.ds(pl.multiple_of(p * piece, piece), piece)
+        down_tiles[p] = lax.dot_general(
+            packed_ref[0, p], dy_ref[...], CONTRACT_ROWS, preferred_element_type=jnp.float32
+        )
+        pltpu.make_async_copy(down_tiles.at[p], down_out.at[where, :], sem.at[2]).start()
+        return carry
+
+    lax.fori_loop(0, pieces, down_step, 0)
+    for a, tiles in enumerate((wide_tiles.at[0], wide_tiles.at[1], down_tiles)):
         pltpu.make_async_copy(tiles, tiles, sem.at[a]).wait()
 
 
 def weight_updates(x_whole, dy_whole, packed):
     rows, width = x_whole.shape
-    hidden_width = packed.shape[2]
-    tall, wide = (next(t for t in (256, 128) if n % t == 0) for n in (hidden_width, width))
+    pieces, piece = packed.shape[1], packed.shape[3]
+    hidden_width = pieces * piece
+    tall = 256 if width % 256 == 0 else 128
     f32 = jnp.float32
+    vmem = pl.BlockSpec(memory_space=pltpu.VMEM)
     hbm = pl.BlockSpec(memory_space=pltpu.HBM)
     return pl.pallas_call(
         update_kernel,
@@ -704,19 +690,14 @@
             jax.ShapeDtypeStruct((width, hidden_width), f32),
             jax.ShapeDtypeStruct((hidden_width, width), f32),
         ),
-        in_specs=[hbm, hbm, hbm],
+        in_specs=[vmem, vmem, vmem],
         out_specs=(hbm, hbm, hbm),
         scratch_shapes=[
-            pltpu.VMEM((rows, width), jnp.bfloat16),
-            pltpu.VMEM((rows, width), jnp.bfloat16),
-            pltpu.VMEM((3, rows, hidden_width), jnp.bfloat16),
-            pltpu.VMEM((width // wide, wide, hidden_width), f32),
-            pltpu.VMEM((width // wide, wide, hidden_width), f32),
-            pltpu.VMEM((hidden_width // tall, tall, width), f32),
-            pltpu.SemaphoreType.DMA((5,)),
+            pltpu.VMEM((2, width // tall, tall, hidden_width), f32),
+            pltpu.VMEM((pieces, piece, width), f32),
             pltpu.SemaphoreType.DMA((3,)),
         ],
-        compiler_params=pltpu.CompilerParams(vmem_limit_bytes=67043328),
+        compiler_params=pltpu.CompilerParams(vmem_limit_bytes=46 * 2**20),
         cost_estimate=pl.CostEstimate(
             flops=6 * rows * width * hidden_width,
             bytes_accessed=12 * width * hidden_width + 2 * rows * (2 * width + 3 * hidden_width),
@@ -734,20 +715,20 @@
     hidden_width = gate_weight.shape[2]
     piece = hidden_width // lax.axis_size("row")
     hbm = pl.BlockSpec(memory_space=pltpu.HBM)
+    vmem = pl.BlockSpec(memory_space=pltpu.VMEM)
     bf16, f32 = jnp.bfloat16, jnp.float32
     dma = pltpu.SemaphoreType.DMA
     block = width // 2
-    far = jax.ShapeDtypeStruct((group, width), bf16)
-    x_whole, dy_whole, packed, own, *far_terms = pl.pallas_call(
+    x_whole, dy_whole, packed, grad = pl.pallas_call(
         relay_kernel,
         out_shape=(
             jax.ShapeDtypeStruct((rows, width), bf16),
             jax.ShapeDtypeStruct((rows, width), bf16),
-            jax.ShapeDtypeStruct((3, rows, hidden_width), bf16),
-            far, far, far, far,
+            jax.ShapeDtypeStruct((3, 4, rows, piece), bf16),
+            jax.ShapeDtypeStruct(held, bf16),
         ),
         in_specs=[hbm] * 5,
-        out_specs=(hbm,) * 7,
+        out_specs=(vmem,) * 4,
         scratch_shapes=[
             pltpu.VMEM((width, hidden_width), bf16),
             pltpu.VMEM((width, hidden_width), bf16),
@@ -755,10 +736,7 @@
             pltpu.VMEM((2, hidden_width, width), bf16),
             pltpu.VMEM((4, *held), bf16),
             pltpu.VMEM((2, 4, local, micro, block), bf16),
-            pltpu.VMEM((rows, width), bf16),
-            pltpu.VMEM((rows, width), bf16),
             pltpu.VMEM((rows, width), f32),
-            pltpu.VMEM((3, 4, rows, piece), bf16),
             pltpu.VMEM((3, 4, rows, piece), bf16),
             pltpu.VMEM((3, 4, rows, piece), bf16),
             pltpu.VMEM((rows, piece), f32),
@@ -768,25 +746,21 @@
             pltpu.VMEM((rows, width), f32),
             pltpu.VMEM((2, 4, group, block), bf16),
             pltpu.VMEM((2, 4, group, block), bf16),
-            pltpu.VMEM((2, local, micro, block), bf16),
             dma((3,)), dma((3,)), dma((9,)), dma((1,)), dma((2,)), dma((2, 2)), dma((2,)), dma((2,)),
-            dma((3, 2)), dma((3, 2)), dma((2,)), dma((2, 4)), dma((2,)), dma((4,)), pltpu.SemaphoreType.REGULAR((2,)),
+            dma((3, 2)), dma((3, 2)), dma((2,)), dma((2, 4)), dma((2,)), pltpu.SemaphoreType.REGULAR((3,)),
         ],
-        compiler_params=pltpu.CompilerParams(collective_id=0, has_side_effects=True, vmem_limit_bytes=60 * 2**20),
+        compiler_params=pltpu.CompilerParams(collective_id=0, has_side_effects=True, vmem_limit_bytes=52000 * 2**10),
     )(
-        panels.transpose(1, 0, 2), out_grad.transpose(1, 0, 2),
-        gate_weight[0], up_weight[0], down_weight[0],
+        *(
+            pltpu.with_memory_space_constraint(array, pltpu.HBM)
+            for array in (
+                panels.transpose(1, 0, 2), out_grad.transpose(1, 0, 2),
+                gate_weight[0], up_weight[0], down_weight[0],
+            )
+        )
     )
-    cols = lax.axis_size("col")
-    arrived = [
-        lax.ppermute(term, "col", [(i, (i + cols - d) % cols) for i in range(cols)])
-        for d, term in zip((1, 2, 3), far_terms, strict=True)
-    ]
     grads = weight_updates(x_whole, dy_whole, packed)
-    grad = dy_whole[:group].astype(f32) + own.astype(f32)
-    for term in arrived:
-        grad = grad + term.astype(f32)
-    grad = grad.astype(bf16).reshape(held).transpose(1, 0, 2)
+    grad = grad.transpose(1, 0, 2)
     return (grad[None], *(g[None] for g in grads))
 
 

time: 75 us -> 72.9 us (0.972)
  starting transfers between devices: 3.28 us -> 0 us
  Pallas kernels: 69.2 us -> 71.5 us
  other arithmetic: 0.93 us -> 0 us
    pallas_call x1, Pallas kernels: 53.1 us -> 56.6 us  [fast_shards(): pl.pallas_call(relay_kernel, out_shape=(jax.ShapeDtypeStruct((rows, width...]
    ppermute x3 -> x0, starting transfers between devices: 3.28 us -> none  [fast_shards(): lax.ppermute(term, 'col', [(i, (i + cols - d) % cols) for i in range(cols)])]
    pallas_call x1, Pallas kernels: 16 us -> 14.9 us  [weight_updates(): pl.pallas_call(update_kernel, out_shape=(jax.ShapeDtypeStruct((width, hid...]
    convert_element_type x1 -> x0, other arithmetic: 0.93 us -> none  [fast_shards(): grad = grad.astype(bf16).reshape(held).transpose(1, 0, 2)]
  transfers between devices with their start and end apart: 3 -> 0, of which waited for: 0 -> 0; matrix products, arithmetic and copies ran while one was open for 0% -> 0% of each run, Pallas kernels for 21% -> 0%
where the time goes in v3:
time: 72.9 us; the launch traced here: 72.7 us
  Pallas kernels  71.5 us (98%)
    pallas_call x1, Pallas kernels, fast_shards(): pl.pallas_call(relay_kernel, out_shape=(jax.ShapeDtypeStruct((rows, width...  56.6 us
    pallas_call x1, Pallas kernels, weight_updates(): pl.pallas_call(update_kernel, out_shape=(jax.ShapeDtypeStruct((width, hid...  14.9 us

profile of v3, /device:TPU:0, one launch (start us, length us, event | category | flops | bytes accessed | tf_op | source)
XLA Modules:
  0.0 72.7 jit_solution(16456431630668108360)
XLA Ops:
  0.6 56.6 %shard_map.84 = (bf16[96,1024]{1,0:T(8,128)(2,1)S(1)}, bf16[96,1024]{1,0:T(8,128)(2,1)S(1)}, bf16[3,4,96,896]{3,2,1,0:T(8,128)(2,1)S(1)}, bf16[12,2,1024]{2,1,0:T(2,128)(2,1)S(1)}) custom-call(bf16[12,2,1024]{2,1,0:T(2,128)(2,1)} %bitcast.17, bf16[12,2,1024]{2,1,0:T(2,128)(2,1)} %bitcast.18, bf16[1024,3584]{1,0:T(8,128)(2,1)} %bitcast.14, ...), custom_call_target="tpu_custom_call" | custom-call | tf_op jit(solution)/shard_map/pallas_call | solution.py:722
  57.2 14.9 %shard_map.85 = (f32[1024,3584]{1,0:T(8,128)}, f32[1024,3584]{1,0:T(8,128)}, f32[3584,1024]{1,0:T(8,128)}) custom-call(bf16[96,1024]{1,0:T(8,128)(2,1)S(1)} %get-tuple-element.12.x_ref, bf16[96,1024]{1,0:T(8,128)(2,1)S(1)} %get-tuple-element.13.dy_ref, bf16[3,4,96,896]{3,2,1,0:T(8,128)(2,1)S(1)} %get-tuple-element.14.packed_ref), custom_call_target="tpu_custom_call" | custom-call | flops 2113929216 | bytes 46497792 | tf_op jit(solution)/shard_map/pallas_call | solution.py:686
  72.1 0.6 copy.10

commit v4 on v3

--- a/solution.py
+++ b/solution.py
@@ -117,7 +117,7 @@
 
 def relay_kernel(
     x_ref, top_ref, gate_ref, up_ref, down_ref,
-    x_whole, dy_whole, spread, result,
+    x_whole, dy_whole, spread, result, ready,
     w_gate, w_up, w_down, turned, x_slots, dy_slots, stage, part_send, part_recv, gate_sum, up_sum, factors, middle,
     branch, branch_send, branch_recv,
     w_sem, in_sem, send_sem, x_recv_sem, dy_recv_sem, via_sem, pair_sem, last_part_sem,
@@ -259,6 +259,15 @@
             branch_send.at[c, d], branch_recv.at[c, d], send_sem.at[5], branch_recv_sem.at[c], (section, row, behind(d))
         )
 
+    def ready_step(j, carry):
+        tall = ready.shape[1]
+        where = pl.ds(pl.multiple_of(j * tall, tall), tall)
+        for p in range(4):
+            ready[j, :, p * width:(p + 1) * width] = lax.dot_general(
+                x_whole[:, where], spread[1, p], CONTRACT_ROWS, preferred_element_type=jnp.float32
+            )
+        return carry
+
     def merge(slots):
         for d in range(4):
             for t in range(local):
@@ -503,9 +512,9 @@
     def branch_step(d, carry):
         @pl.when(d == 1)
         def _():
-            for h in range(2):
-                relay_grads(h)
+            relay_grads(0)
             partner_go(1)
+            relay_grads(1)
             received(spread.at[2, row_peer(1)], second_sem.at[2, 0])
 
         @pl.when(d == 2)
@@ -595,7 +604,6 @@
         factor_rows(0, 3)
         for i in range(4):
             cross_sum(i)
-        partner_go(2)
         received(spread.at[pl.ds(1, 2), row_peer(3)], onward_sem.at[1])
         factor_rows(3, 1)
         sent(spread.at[pl.ds(1, 2), pl.ds(1, 2)], 3)
@@ -605,6 +613,14 @@
         lax.fori_loop(0, 2, last_cross_step, 0)
 
     send_branch(1)
+
+    @pl.when(is_top)
+    def _():
+        spread_hidden()
+
+    @pl.when(is_bottom)
+    def _():
+        lax.fori_loop(0, ready.shape[0], ready_step, 0)
 
     for c in range(2):
         cols = slice(c * block, (c + 1) * block)
@@ -623,9 +639,8 @@
 
     @pl.when(is_top)
     def _():
-        pl.semaphore_wait(go_sem.at[2], 1)
-        spread_hidden()
         relay_hidden()
+        lax.fori_loop(0, ready.shape[0], ready_step, 0)
         finish_hidden()
         sent(dy_slots.at[:, pl.ds(1, 3)], 1)
         sent(dy_slots, 6)
@@ -642,44 +657,55 @@
     sent(branch_send.at[:, pl.ds(1, 3)], 5)
     sent(x_slots.at[pl.ds(1, 3)], 0)
 
-def update_kernel(x_ref, dy_ref, packed_ref, gate_out, up_out, down_out, wide_tiles, down_tiles, sem):
+def update_kernel(x_ref, dy_ref, packed_ref, ready_ref, gate_out, up_out, down_out, wide_tiles, down_tiles, sem, ready_sem):
     pieces, rows, piece = packed_ref.shape[1:]
-    tall = wide_tiles.shape[2]
+    tall = wide_tiles.shape[1]
+    made, blocks = ready_ref.shape[0], x_ref.shape[1] // tall
+
+    def where_of(j):
+        return pl.ds(j * tall if isinstance(j, int) else pl.multiple_of(j * tall, tall), tall)
+
+    ready_copies = [
+        pltpu.make_async_copy(ready_ref.at[j], gate_out.at[where_of(j), :], ready_sem.at[j]) for j in range(made)
+    ]
+    for copy in ready_copies:
+        copy.start()
 
     def wide_step(k, carry):
-        a = k // wide_tiles.shape[1]
-        j = k % wide_tiles.shape[1]
-        where = pl.ds(pl.multiple_of(j * tall, tall), tall)
-
+        a = (k + made) // blocks
+        where = where_of((k + made) % blocks)
         for p in range(pieces):
-            wide_tiles[a, j, :, p * piece:(p + 1) * piece] = lax.dot_general(
+            wide_tiles[k, :, p * piece:(p + 1) * piece] = lax.dot_general(
                 x_ref[:, where], packed_ref[1 + a, p], CONTRACT_ROWS, preferred_element_type=jnp.float32
             )
         for b, target in enumerate((gate_out, up_out)):
             @pl.when(a == b)
             def _():
-                pltpu.make_async_copy(wide_tiles.at[b, j], target.at[where, :], sem.at[b]).start()
-        return carry
-
-    lax.fori_loop(0, 2 * wide_tiles.shape[1], wide_step, 0)
+                pltpu.make_async_copy(wide_tiles.at[k], target.at[where, :], sem.at[0]).start()
+        return carry
+
+    lax.fori_loop(0, wide_tiles.shape[0], wide_step, 0)
+
     def down_step(p, carry):
         where = pl.ds(pl.multiple_of(p * piece, piece), piece)
         down_tiles[p] = lax.dot_general(
             packed_ref[0, p], dy_ref[...], CONTRACT_ROWS, preferred_element_type=jnp.float32
         )
-        pltpu.make_async_copy(down_tiles.at[p], down_out.at[where, :], sem.at[2]).start()
+        pltpu.make_async_copy(down_tiles.at[p], down_out.at[where, :], sem.at[1]).start()
         return carry
 
     lax.fori_loop(0, pieces, down_step, 0)
-    for a, tiles in enumerate((wide_tiles.at[0], wide_tiles.at[1], down_tiles)):
+    for copy in ready_copies:
+        copy.wait()
+    for a, tiles in enumerate((wide_tiles, down_tiles)):
         pltpu.make_async_copy(tiles, tiles, sem.at[a]).wait()
 
 
-def weight_updates(x_whole, dy_whole, packed):
+def weight_updates(x_whole, dy_whole, packed, ready):
     rows, width = x_whole.shape
     pieces, piece = packed.shape[1], packed.shape[3]
     hidden_width = pieces * piece
-    tall = 256 if width % 256 == 0 else 128
+    made, tall = ready.shape[:2]
     f32 = jnp.float32
     vmem = pl.BlockSpec(memory_space=pltpu.VMEM)
     hbm = pl.BlockSpec(memory_space=pltpu.HBM)
@@ -690,20 +716,21 @@
             jax.ShapeDtypeStruct((width, hidden_width), f32),
             jax.ShapeDtypeStruct((hidden_width, width), f32),
         ),
-        in_specs=[vmem, vmem, vmem],
+        in_specs=[vmem, vmem, vmem, vmem],
         out_specs=(hbm, hbm, hbm),
         scratch_shapes=[
-            pltpu.VMEM((2, width // tall, tall, hidden_width), f32),
+            pltpu.VMEM((2 * width // tall - made, tall, hidden_width), f32),
             pltpu.VMEM((pieces, piece, width), f32),
-            pltpu.SemaphoreType.DMA((3,)),
+            pltpu.SemaphoreType.DMA((2,)),
+            pltpu.SemaphoreType.DMA((made,)),
         ],
-        compiler_params=pltpu.CompilerParams(vmem_limit_bytes=46 * 2**20),
+        compiler_params=pltpu.CompilerParams(vmem_limit_bytes=44 * 2**20),
         cost_estimate=pl.CostEstimate(
             flops=6 * rows * width * hidden_width,
             bytes_accessed=12 * width * hidden_width + 2 * rows * (2 * width + 3 * hidden_width),
             transcendentals=0,
         ),
-    )(x_whole, dy_whole, packed)
+    )(x_whole, dy_whole, packed, ready)
 
 
 def fast_shards(section_inputs, out_grad, gate_weight, up_weight, down_weight):
@@ -719,16 +746,18 @@
     bf16, f32 = jnp.bfloat16, jnp.float32
     dma = pltpu.SemaphoreType.DMA
     block = width // 2
-    x_whole, dy_whole, packed, grad = pl.pallas_call(
+    tall = 256 if width % 256 == 0 else 128
+    x_whole, dy_whole, packed, grad, ready = pl.pallas_call(
         relay_kernel,
         out_shape=(
             jax.ShapeDtypeStruct((rows, width), bf16),
             jax.ShapeDtypeStruct((rows, width), bf16),
             jax.ShapeDtypeStruct((3, 4, rows, piece), bf16),
             jax.ShapeDtypeStruct(held, bf16),
+            jax.ShapeDtypeStruct((1, tall, hidden_width), f32),
         ),
         in_specs=[hbm] * 5,
-        out_specs=(vmem,) * 4,
+        out_specs=(vmem,) * 5,
         scratch_shapes=[
             pltpu.VMEM((width, hidden_width), bf16),
             pltpu.VMEM((width, hidden_width), bf16),
@@ -747,9 +776,9 @@
             pltpu.VMEM((2, 4, group, block), bf16),
             pltpu.VMEM((2, 4, group, block), bf16),
             dma((3,)), dma((3,)), dma((9,)), dma((1,)), dma((2,)), dma((2, 2)), dma((2,)), dma((2,)),
-            dma((3, 2)), dma((3, 2)), dma((2,)), dma((2, 4)), dma((2,)), pltpu.SemaphoreType.REGULAR((3,)),
+            dma((3, 2)), dma((3, 2)), dma((2,)), dma((2, 4)), dma((2,)), pltpu.SemaphoreType.REGULAR((2,)),
         ],
-        compiler_params=pltpu.CompilerParams(collective_id=0, has_side_effects=True, vmem_limit_bytes=52000 * 2**10),
+        compiler_params=pltpu.CompilerParams(collective_id=0, has_side_effects=True, vmem_limit_bytes=46800 * 2**10),
     )(
         *(
             pltpu.with_memory_space_constraint(array, pltpu.HBM)
@@ -759,7 +788,7 @@
             )
         )
     )
-    grads = weight_updates(x_whole, dy_whole, packed)
+    grads = weight_updates(x_whole, dy_whole, packed, ready)
     grad = grad.transpose(1, 0, 2)
     return (grad[None], *(g[None] for g in grads))
 

time: 72.9 us -> 71.8 us (0.985)
  Pallas kernels: 71.5 us -> 70.4 us
where the time goes in v4:
time: 71.8 us; the launch traced here: 71.7 us
  Pallas kernels  70.4 us (98%)
    pallas_call x1, Pallas kernels, fast_shards(): pl.pallas_call(relay_kernel, out_shape=(jax.ShapeDtypeStruct((rows, width...  56.2 us
    pallas_call x1, Pallas kernels, weight_updates(): pl.pallas_call(update_kernel, out_shape=(jax.ShapeDtypeStruct((width, hid...  14.2 us

profile of v4, /device:TPU:0, one launch (start us, length us, event | category | flops | bytes accessed | tf_op | source)
XLA Modules:
  0.0 71.7 jit_solution(9340949544542057856)
XLA Ops:
  0.6 56.2 %shard_map.84 = (bf16[96,1024]{1,0:T(8,128)(2,1)S(1)}, bf16[96,1024]{1,0:T(8,128)(2,1)S(1)}, bf16[3,4,96,896]{3,2,1,0:T(8,128)(2,1)S(1)}, bf16[12,2,1024]{2,1,0:T(2,128)(2,1)S(1)}, f32[1,256,3584]{2,1,0:T(8,128)S(1)}) custom-call(bf16[12,2,1024]{2,1,0:T(2,128)(2,1)} %bitcast.17, bf16[12,2,1024]{2,1,0:T(2,128)(2,1)} %bitcast.18, bf16[1024,3584]{1,0:T(8,128)(2,1)} %bitcast.14, ...), custom_call_target="tpu_custom_call" | custom-call | tf_op jit(solution)/shard_map/pallas_call | solution.py:750
  56.8 14.2 %shard_map.85 = (f32[1024,3584]{1,0:T(8,128)}, f32[1024,3584]{1,0:T(8,128)}, f32[3584,1024]{1,0:T(8,128)}) custom-call(bf16[96,1024]{1,0:T(8,128)(2,1)S(1)} %get-tuple-element.13.x_ref, bf16[96,1024]{1,0:T(8,128)(2,1)S(1)} %get-tuple-element.14.dy_ref, bf16[3,4,96,896]{3,2,1,0:T(8,128)(2,1)S(1)} %get-tuple-element.15.packed_ref, ...), custom_call_target="tpu_custom_call" | custom-call | flops 2113929216 | bytes 46497792 | tf_op jit(solution)/shard_map/pallas_call | solution.py:712
  71.1 0.6 copy.10

commit v5 on v4

--- a/solution.py
+++ b/solution.py
@@ -657,7 +657,10 @@
     sent(branch_send.at[:, pl.ds(1, 3)], 5)
     sent(x_slots.at[pl.ds(1, 3)], 0)
 
-def update_kernel(x_ref, dy_ref, packed_ref, ready_ref, gate_out, up_out, down_out, wide_tiles, down_tiles, sem, ready_sem):
+def update_kernel(
+    x_ref, dy_ref, packed_ref, ready_ref, grad_ref, gate_out, up_out, down_out, grad_out,
+    wide_tiles, down_tiles, sem, ready_sem, grad_sem,
+):
     pieces, rows, piece = packed_ref.shape[1:]
     tall = wide_tiles.shape[1]
     made, blocks = ready_ref.shape[0], x_ref.shape[1] // tall
@@ -670,6 +673,8 @@
     ]
     for copy in ready_copies:
         copy.start()
+    grad_copy = pltpu.make_async_copy(grad_ref, grad_out, grad_sem)
+    grad_copy.start()
 
     def wide_step(k, carry):
         a = (k + made) // blocks
@@ -697,11 +702,12 @@
     lax.fori_loop(0, pieces, down_step, 0)
     for copy in ready_copies:
         copy.wait()
+    grad_copy.wait()
     for a, tiles in enumerate((wide_tiles, down_tiles)):
         pltpu.make_async_copy(tiles, tiles, sem.at[a]).wait()
 
 
-def weight_updates(x_whole, dy_whole, packed, ready):
+def weight_updates(x_whole, dy_whole, packed, ready, grad):
     rows, width = x_whole.shape
     pieces, piece = packed.shape[1], packed.shape[3]
     hidden_width = pieces * piece
@@ -715,14 +721,16 @@
             jax.ShapeDtypeStruct((width, hidden_width), f32),
             jax.ShapeDtypeStruct((width, hidden_width), f32),
             jax.ShapeDtypeStruct((hidden_width, width), f32),
+            jax.ShapeDtypeStruct(grad.shape, grad.dtype),
         ),
-        in_specs=[vmem, vmem, vmem, vmem],
-        out_specs=(hbm, hbm, hbm),
+        in_specs=[vmem] * 5,
+        out_specs=(hbm,) * 4,
         scratch_shapes=[
             pltpu.VMEM((2 * width // tall - made, tall, hidden_width), f32),
             pltpu.VMEM((pieces, piece, width), f32),
             pltpu.SemaphoreType.DMA((2,)),
             pltpu.SemaphoreType.DMA((made,)),
+            pltpu.SemaphoreType.DMA,
         ],
         compiler_params=pltpu.CompilerParams(vmem_limit_bytes=44 * 2**20),
         cost_estimate=pl.CostEstimate(
@@ -730,7 +738,7 @@
             bytes_accessed=12 * width * hidden_width + 2 * rows * (2 * width + 3 * hidden_width),
             transcendentals=0,
         ),
-    )(x_whole, dy_whole, packed, ready)
+    )(x_whole, dy_whole, packed, ready, grad)
 
 
 def fast_shards(section_inputs, out_grad, gate_weight, up_weight, down_weight):
@@ -788,7 +796,7 @@
             )
         )
     )
-    grads = weight_updates(x_whole, dy_whole, packed, ready)
+    *grads, grad = weight_updates(x_whole, dy_whole, packed, ready, grad)
     grad = grad.transpose(1, 0, 2)
     return (grad[None], *(g[None] for g in grads))
 

time: 71.8 us -> 71.2 us (level)
  no operation moved by 1% of the time
where the time goes in v5:
time: 71.2 us; the launch traced here: 71.1 us
  Pallas kernels  70.4 us (99%)
    pallas_call x1, Pallas kernels, fast_shards(): pl.pallas_call(relay_kernel, out_shape=(jax.ShapeDtypeStruct((rows, width...  56.2 us
    pallas_call x1, Pallas kernels, weight_updates(): pl.pallas_call(update_kernel, out_shape=(jax.ShapeDtypeStruct((width, hid...  14.2 us

profile of v5, /device:TPU:0, one launch (start us, length us, event | category | flops | bytes accessed | tf_op | source)
XLA Modules:
  0.0 71.1 jit_solution(7740597514302423425)
XLA Ops:
  0.6 56.2 %shard_map.84 = (bf16[96,1024]{1,0:T(8,128)(2,1)S(1)}, bf16[96,1024]{1,0:T(8,128)(2,1)S(1)}, bf16[3,4,96,896]{3,2,1,0:T(8,128)(2,1)S(1)}, bf16[12,2,1024]{2,1,0:T(2,128)(2,1)S(1)}, f32[1,256,3584]{2,1,0:T(8,128)S(1)}) custom-call(bf16[12,2,1024]{2,1,0:T(2,128)(2,1)} %bitcast.16, bf16[12,2,1024]{2,1,0:T(2,128)(2,1)} %bitcast.17, bf16[1024,3584]{1,0:T(8,128)(2,1)} %bitcast.13, ...), custom_call_target="tpu_custom_call" | custom-call | tf_op jit(solution)/shard_map/pallas_call | solution.py:758
  56.8 14.2 %shard_map.85 = (f32[1024,3584]{1,0:T(8,128)}, f32[1024,3584]{1,0:T(8,128)}, f32[3584,1024]{1,0:T(8,128)}, bf16[12,2,1024]{2,1,0:T(2,128)(2,1)}) custom-call(bf16[96,1024]{1,0:T(8,128)(2,1)S(1)} %get-tuple-element.13.x_ref, bf16[96,1024]{1,0:T(8,128)(2,1)S(1)} %get-tuple-element.14.dy_ref, bf16[3,4,96,896]{3,2,1,0:T(8,128)(2,1)S(1)} %get-tuple-element.15.packed_ref, ...), custom_call_target="tpu_custom_call" | custom-call | flops 2113929216 | bytes 46497792 | tf_op jit(solution)/shard_map/pallas_call | solution.py:718
